TPU v7x, 128 devices: a whole 4x4x4 slice. The times are simulated.
128 devices in a mesh: segment: 2 (over core), gx: 8 (over z_hi, x), gy: 4 (over y), gz: 2 (over z_lo).
Axes of the slice: x: 4, y: 4, z: 4 (z_hi: 2, z_lo: 2; z = z_hi * 2 + z_lo), core: 2. Of those that a mesh axis runs over, the one named last changes fastest.
Arguments:
- features: bfloat16 [2, 16, 32, 128, 256], P(None, None, 'gx', 'gy', 'gz'), may hold values from -6 to 6
- weights: bfloat16 [2, 2, 16, 16, 3, 3, 3], P('segment'), may hold values from -0.4375 to 0.4375
- biases: bfloat16 [2, 2, 16], P('segment'), may hold values from -3 to 3
Outputs:
- section_out: bfloat16 [2, 2, 16, 32, 128, 256], P('segment', None, None, 'gx', 'gy', 'gz')
All inputs are finite; a program needn't handle non-finite values.
Results may differ from a plain program's by a relative error of at most 0.0054.
Values may be sent and summed in bfloat16 or wider, within the bound.
A program may use at most 64 MiB of HBM per device.

v0:
```python
import math

import jax
import jax.numpy as jnp
from jax import lax
from jax.sharding import PartitionSpec as P


def with_halo(value, sides, width):
    for axis, dim in sides:
        size, length = (lax.axis_size(axis), value.shape[dim])
        up = [(i, (i + 1) % size) for i in range(size - 1)]
        down = [(j, i) for i, j in up]
        last = lax.slice_in_dim(value, length - width, length, axis=dim)
        initial = lax.slice_in_dim(value, 0, width, axis=dim)
        before = lax.ppermute(last, axis, up)
        after = lax.ppermute(initial, axis, down)
        value = jnp.concatenate([before, value, after], axis=dim)
    return value


def side_by_side(arrays, axis, dim, along):
    widths = [math.prod(a.shape[along:]) for a in arrays]
    both = jnp.concatenate(
        [a.reshape(*a.shape[:along], w) for a, w in zip(arrays, widths)], axis=along
    )
    out = lax.all_gather(both, axis, axis=dim, tiled=True)
    blocks = jnp.split(out, [sum(widths[:k]) for k in range(1, len(widths))], axis=along)
    return tuple((b.reshape(*out.shape[:along], *a.shape[along:]) for a, b in zip(arrays, blocks)))


def band_table(width):
    source = lax.broadcasted_iota(jnp.int32, (width + 2, 3, width), 0)
    offsets = lax.broadcasted_iota(jnp.int32, (width + 2, 3, width), 1)
    target = lax.broadcasted_iota(jnp.int32, (width + 2, 3, width), 2)
    return jnp.where(source == target + offsets, 1.0, 0.0).astype(jnp.bfloat16)


def convolve(field, kernel, offset):
    padded = with_halo(field, (("gx", 1), ("gy", 2), ("gz", 3)), 1)
    depth = field.shape[1]
    height = field.shape[2]
    width = field.shape[3]
    shifted = jnp.einsum(
        "cxyw,wdz->dcxyz", padded, band_table(width), preferred_element_type=jnp.float32
    ).astype(jnp.bfloat16)
    linear = jnp.zeros((kernel.shape[0], depth, height, width), jnp.float32)
    for step_x in range(3):
        for step_y in range(3):
            slab = shifted[:, :, step_x : step_x + depth, step_y : step_y + height, :]
            taps = kernel[:, :, step_x, step_y, :]
            linear = linear + jnp.einsum(
                "oid,dixyz->oxyz", taps, slab, preferred_element_type=jnp.float32
            )
    summed = linear + offset.astype(jnp.float32)[:, None, None, None]
    return jnp.where(summed > 0, summed, 0.2 * summed).astype(jnp.bfloat16)


def section_pass(field, kernels, offsets):
    return convolve(convolve(field, kernels[0], offsets[0]), kernels[1], offsets[1])


def shards(features, weights, biases):
    section = lax.axis_index("segment")
    micro_count = features.shape[0]
    all_kernels, all_offsets = side_by_side((weights, biases), "segment", 0, 3)
    half_count = micro_count // 2
    my_batches = lax.dynamic_slice_in_dim(features, section * half_count, half_count, 0)
    hidden = section_pass(my_batches[0], all_kernels[0], all_offsets[0])
    first_list = [hidden]
    hidden = section_pass(hidden, all_kernels[1], all_offsets[1])
    second_list = [hidden]
    stacked = jnp.stack([jnp.stack(first_list), jnp.stack(second_list)])
    return lax.all_to_all(stacked, "segment", split_axis=0, concat_axis=1, tiled=True)


def solution(mesh):
    placed = (
        P(None, None, "gx", "gy", "gz"),
        P("segment", None, None, None, None, None, None),
        P("segment", None, None),
    )
    return jax.shard_map(
        shards,
        mesh=mesh,
        in_specs=placed,
        out_specs=P("segment", None, None, "gx", "gy", "gz"),
        check_vma=False,
    )
```

profile of v0, /device:TPU:7, one launch (start us, length us, event | category | flops | bytes accessed | tf_op | source)
XLA Modules:
  0.0 207.1 jit_solution(3466477335191406419)
XLA Ops:
  0.0 1.2 copy-done
  1.3 5.4 %collective-permute-start = (bf16[16,1,32,128]{3,2,1,0:T(8,128)(2,1)S(1)}, bf16[16,1,32,128]{3,2,1,0:T(8,128)(2,1)S(1)}, u32[]{:S(2)}, u32[]{:S(2)}) collective-permute-start(bf16[16,1,32,128]{3,2,1,0:T(8,128)(2,1)S(1)} %get-tuple-element.67), channel_id=1, source_target_pairs={{0,8},{8,16},{16,24},{24,32},{32,40},{40,48},{48,56},{1,9},{9,17},... | collective-permute-start | bytes 393224 | tf_op jit(solution)/shard_map/ppermute | solution.py:16
  6.7 1.9 collective-permute-start.1
  9.1 2.5 %all_gather.3 = bf16[2,2,16,433]{3,2,1,0:T(8,128)(2,1)S(1)} all-gather(bf16[1,2,16,433]{3,2,1,0:T(8,128)(2,1)S(1)} %pad_maximum_fusion.11), channel_id=1, replica_groups=mesh['segment'=2,'gx'=8,'gy'=4,'gz'=2] {'segment'}, dimensions={0}, use_global_device_ids=true | all-gather | bytes 83136 | tf_op jit(solution)/shard_map/all_gather | solution.py:27
  11.8 4.2 %collective-permute-done.1 = bf16[16,1,32,128]{3,2,1,0:T(8,128)(2,1)S(1)} collective-permute-done((bf16[16,1,32,128]{3,2,1,0:T(8,128)(2,1)S(1)}, bf16[16,1,32,128]{3,2,1,0:T(8,128)(2,1)S(1)}, u32[]{:S(2)}, u32[]{:S(2)}) %collective-permute-start.1) | collective-permute-done | bytes 131104 | tf_op jit(solution)/shard_map/ppermute | solution.py:17
  16.1 3.2 %collective-permute-start.2 = (bf16[16,6,1,128]{3,2,1,0:T(2,128)(2,1)S(1)}, bf16[16,6,1,128]{3,2,1,0:T(2,128)(2,1)S(1)}, u32[]{:S(2)}, u32[]{:S(2)}) collective-permute-start(bf16[16,6,1,128]{3,2,1,0:T(2,128)(2,1)S(1)} %get-tuple-element.59), channel_id=1, source_target_pairs={{0,2},{2,4},{4,6},{1,3},{3,5},{5,7},{8,10},{10,12},{12,14},{9,11},... | collective-permute-start | bytes 73736 | tf_op jit(solution)/shard_map/ppermute | solution.py:16
  19.3 1.3 collective-permute-start.3
  20.7 3.5 %collective-permute-done.3 = bf16[16,6,1,128]{3,2,1,0:T(2,128)(2,1)S(1)} collective-permute-done((bf16[16,6,1,128]{3,2,1,0:T(2,128)(2,1)S(1)}, bf16[16,6,1,128]{3,2,1,0:T(2,128)(2,1)S(1)}, u32[]{:S(2)}, u32[]{:S(2)}) %collective-permute-start.3) | collective-permute-done | bytes 24608 | tf_op jit(solution)/shard_map/ppermute | solution.py:17
  25.8 2.6 %collective-permute-start.4 = (bf16[16,6,34,1]{2,0,3,1:T(8,128)(2,1)S(1)}, bf16[16,6,34,1]{2,0,3,1:T(8,128)(2,1)S(1)}, u32[]{:S(2)}, u32[]{:S(2)}) collective-permute-start(bf16[16,6,34,1]{2,0,3,1:T(8,128)(2,1)S(1)} %copy.228), channel_id=1, source_target_pairs={{0,1},{2,3},{4,5},{6,7},{8,9},{10,11},{12,13},{14,15},{16,17},{18,... | collective-permute-start | bytes 19592 | tf_op jit(solution)/shard_map/ppermute | solution.py:16
  29.1 1.3 collective-permute-start.5
  32.2 1.5 collective-permute-done.5
  34.4 2.9 %convert_bitcast_fusion.3 = bf16[3,16,6,34,128]{4,3,2,1,0:T(8,128)(2,1)S(1)} fusion(bf16[16,6,34,1]{3,2,1,0:T(8,128)(2,1)S(1)} %copy.231, bf16[16,6,1,128]{3,2,1,0:T(2,128)(2,1)S(1)} %collective-permute-done.3, bf16[16,1,32,128]{3,2,1,0:T(8,128)(2,1)S(1)} %collective-permute-done.1, bf16[16,4,32,128]{3,2,1,0:T(8,128)(2,1)S(1)} %dynamic-slice_bitcast_fusion, ...), kind=kOutput, calls=%fused_computation.7 | convolution fusion | flops 333271296 | bytes 3355392 | tf_op jit(solution)/shard_map/cxyw,wdz->dcxyz/dot_general | solution.py:44
  37.4 3.7 %fusion.390 = (bf16[3,16,4,32,128]{4,3,2,1,0:T(8,128)(2,1)S(1)}, bf16[3,16,4,32,128]{4,3,2,1,0:T(8,128)(2,1)S(1)}, bf16[3,16,4,32,128]{4,3,2,1,0:T(8,128)(2,1)S(...) fusion(bf16[3,16,6,34,128]{4,3,2,1,0:T(8,128)(2,1)S(1)} %conver, ...), kind=kLoop, calls=%fused_computation.261 | loop fusion | bytes 28311552 | tf_op jit(solution)/shard_map/slice | solution.py:50
  42.1 1.1 fusion.311
  44.2 1.1 fusion.305
  45.3 1.1 fusion.302
  46.4 1.1 fusion.299
  48.5 1.1 fusion.293
  49.6 1.1 fusion.314
  50.7 3.7 %collective-permute-start.6 = (bf16[16,1,32,128]{3,0,2,1:T(8,128)(2,1)S(1)}, bf16[16,1,32,128]{3,0,2,1:T(8,128)(2,1)S(1)}, u32[]{:S(2)}, u32[]{:S(2)}) collective-permute-start(bf16[16,1,32,128]{3,0,2,1:T(8,128)(2,1)S(1)} %get-tuple-element.65), channel_id=1, source_target_pairs={{0,8},{8,16},{16,24},{24,32},{32,40},{40,48},{48,56},{1,9},{9,17},... | collective-permute-start | bytes 393224 | tf_op jit(solution)/shard_map/ppermute | solution.py:16
  54.4 1.9 collective-permute-start.7
  56.5 7.3 %collective-permute-done.7 = bf16[16,1,32,128]{3,0,2,1:T(8,128)(2,1)S(1)} collective-permute-done((bf16[16,1,32,128]{3,0,2,1:T(8,128)(2,1)S(1)}, bf16[16,1,32,128]{3,0,2,1:T(8,128)(2,1)S(1)}, u32[]{:S(2)}, u32[]{:S(2)}) %collective-permute-start.7) | collective-permute-done | bytes 131104 | tf_op jit(solution)/shard_map/ppermute | solution.py:17
  63.8 3.2 %collective-permute-start.8 = (bf16[16,6,1,128]{3,0,2,1:T(8,128)(2,1)S(1)}, bf16[16,6,1,128]{3,0,2,1:T(8,128)(2,1)S(1)}, u32[]{:S(2)}, u32[]{:S(2)}) collective-permute-start(bf16[16,6,1,128]{3,0,2,1:T(8,128)(2,1)S(1)} %get-tuple-element.57), channel_id=1, source_target_pairs={{0,2},{2,4},{4,6},{1,3},{3,5},{5,7},{8,10},{10,12},{12,14},{9,11},... | collective-permute-start | bytes 73736 | tf_op jit(solution)/shard_map/ppermute | solution.py:16
  67.0 1.5 collective-permute-start.9
  68.7 2.8 %collective-permute-done.9 = bf16[16,6,1,128]{3,0,2,1:T(8,128)(2,1)S(1)} collective-permute-done((bf16[16,6,1,128]{3,0,2,1:T(8,128)(2,1)S(1)}, bf16[16,6,1,128]{3,0,2,1:T(8,128)(2,1)S(1)}, u32[]{:S(2)}, u32[]{:S(2)}) %collective-permute-start.9) | collective-permute-done | bytes 24608 | tf_op jit(solution)/shard_map/ppermute | solution.py:17
  73.0 1.9 collective-permute-start.10
  75.7 1.3 collective-permute-start.11
  78.8 1.5 collective-permute-done.11
  81.1 1.9 pad_maximum_fusion
  83.0 1.4 convert_bitcast_fusion.2
  84.4 4.1 %fusion.389 = (bf16[3,16,4,32,128]{4,3,2,1,0:T(8,128)(2,1)S(1)}, bf16[3,16,4,32,128]{4,3,2,1,0:T(8,128)(2,1)S(1)}, bf16[3,16,4,32,128]{4,3,2,1,0:T(8,128)(2,1)S(...) fusion(bf16[3,16,6,34,128]{4,3,2,1,0:T(8,128)(2,1)S(1)} %conver, ...), kind=kLoop, calls=%fused_computation.260 | loop fusion | bytes 28311552 | tf_op jit(solution)/shard_map/slice | solution.py:50
  89.5 1.1 fusion.282
  90.6 1.1 fusion.279
  91.6 1.1 fusion.276
  93.8 1.1 fusion.270
  97.0 1.1 fusion.317
  98.1 2.1 %collective-permute-start.12 = (bf16[16,1,32,128]{3,0,2,1:T(8,128)(2,1)S(1)}, bf16[16,1,32,128]{3,0,2,1:T(8,128)(2,1)S(1)}, u32[]{:S(2)}, u32[]{:S(2)}) collective-permute-start(bf16[16,1,32,128]{3,0,2,1:T(8,128)(2,1)S(1)} %get-tuple-element.63), channel_id=1, source_target_pairs={{0,8},{8,16},{16,24},{24,32},{32,40},{40,48},{48,56},{1,9},{9,17},... | collective-permute-start | bytes 393224 | tf_op jit(solution)/shard_map/ppermute | solution.py:16
  100.3 3.2 %collective-permute-start.13 = (bf16[16,1,32,128]{3,0,2,1:T(8,128)(2,1)S(1)}, bf16[16,1,32,128]{3,0,2,1:T(8,128)(2,1)S(1)}, u32[]{:S(2)}, u32[]{:S(2)}) collective-permute-start(bf16[16,1,32,128]{3,0,2,1:T(8,128)(2,1)S(1)} %get-tuple-element.64), channel_id=1, source_target_pairs={{8,0},{16,8},{24,16},{32,24},{40,32},{48,40},{56,48},{9,1},{17,9},... | collective-permute-start | bytes 393224 | tf_op jit(solution)/shard_map/ppermute | solution.py:17
  103.9 5.7 %collective-permute-done.13 = bf16[16,1,32,128]{3,0,2,1:T(8,128)(2,1)S(1)} collective-permute-done((bf16[16,1,32,128]{3,0,2,1:T(8,128)(2,1)S(1)}, bf16[16,1,32,128]{3,0,2,1:T(8,128)(2,1)S(1)}, u32[]{:S(2)}, u32[]{:S(2)}) %collective-permute-start.13) | collective-permute-done | bytes 131104 | tf_op jit(solution)/shard_map/ppermute | solution.py:17
  109.6 2.9 %collective-permute-start.14 = (bf16[16,6,1,128]{3,0,2,1:T(8,128)(2,1)S(1)}, bf16[16,6,1,128]{3,0,2,1:T(8,128)(2,1)S(1)}, u32[]{:S(2)}, u32[]{:S(2)}) collective-permute-start(bf16[16,6,1,128]{3,0,2,1:T(8,128)(2,1)S(1)} %get-tuple-element.55), channel_id=1, source_target_pairs={{0,2},{2,4},{4,6},{1,3},{3,5},{5,7},{8,10},{10,12},{12,14},{9,11},... | collective-permute-start | bytes 73736 | tf_op jit(solution)/shard_map/ppermute | solution.py:16
  112.5 1.3 collective-permute-start.15
  114.1 3.2 %collective-permute-done.15 = bf16[16,6,1,128]{3,0,2,1:T(8,128)(2,1)S(1)} collective-permute-done((bf16[16,6,1,128]{3,0,2,1:T(8,128)(2,1)S(1)}, bf16[16,6,1,128]{3,0,2,1:T(8,128)(2,1)S(1)}, u32[]{:S(2)}, u32[]{:S(2)}) %collective-permute-start.15) | collective-permute-done | bytes 24608 | tf_op jit(solution)/shard_map/ppermute | solution.py:17
  118.7 2.1 %collective-permute-start.16 = (bf16[16,6,34,1]{2,0,3,1:T(8,128)(2,1)S(1)}, bf16[16,6,34,1]{2,0,3,1:T(8,128)(2,1)S(1)}, u32[]{:S(2)}, u32[]{:S(2)}) collective-permute-start(bf16[16,6,34,1]{2,0,3,1:T(8,128)(2,1)S(1)} %copy.275), channel_id=1, source_target_pairs={{0,1},{2,3},{4,5},{6,7},{8,9},{10,11},{12,13},{14,15},{16,17},{18,... | collective-permute-start | bytes 19592 | tf_op jit(solution)/shard_map/ppermute | solution.py:16
  121.7 1.5 collective-permute-start.17
  124.9 1.3 collective-permute-done.17
  127.1 1.9 pad_maximum_fusion.1
  129.0 1.4 convert_bitcast_fusion.1
  130.3 3.7 %fusion.388 = (bf16[3,16,4,32,128]{4,3,2,1,0:T(8,128)(2,1)S(1)}, bf16[3,16,4,32,128]{4,3,2,1,0:T(8,128)(2,1)S(1)}, bf16[3,16,4,32,128]{4,3,2,1,0:T(8,128)(2,1)S(...) fusion(bf16[3,16,6,34,128]{4,3,2,1,0:T(8,128)(2,1)S(1)} %conver, ...), kind=kLoop, calls=%fused_computation.259 | loop fusion | bytes 28311552 | tf_op jit(solution)/shard_map/slice | solution.py:50
  142.5 1.1 fusion.320
  143.6 2.1 %collective-permute-start.18 = (bf16[16,1,32,128]{3,0,2,1:T(8,128)(2,1)S(1)}, bf16[16,1,32,128]{3,0,2,1:T(8,128)(2,1)S(1)}, u32[]{:S(2)}, u32[]{:S(2)}) collective-permute-start(bf16[16,1,32,128]{3,0,2,1:T(8,128)(2,1)S(1)} %get-tuple-element.61), channel_id=1, source_target_pairs={{0,8},{8,16},{16,24},{24,32},{32,40},{40,48},{48,56},{1,9},{9,17},... | collective-permute-start | bytes 393224 | tf_op jit(solution)/shard_map/ppermute | solution.py:16
  145.7 3.2 %collective-permute-start.19 = (bf16[16,1,32,128]{3,0,2,1:T(8,128)(2,1)S(1)}, bf16[16,1,32,128]{3,0,2,1:T(8,128)(2,1)S(1)}, u32[]{:S(2)}, u32[]{:S(2)}) collective-permute-start(bf16[16,1,32,128]{3,0,2,1:T(8,128)(2,1)S(1)} %get-tuple-element.62), channel_id=1, source_target_pairs={{8,0},{16,8},{24,16},{32,24},{40,32},{48,40},{56,48},{9,1},{17,9},... | collective-permute-start | bytes 393224 | tf_op jit(solution)/shard_map/ppermute | solution.py:17
  149.3 5.7 %collective-permute-done.19 = bf16[16,1,32,128]{3,0,2,1:T(8,128)(2,1)S(1)} collective-permute-done((bf16[16,1,32,128]{3,0,2,1:T(8,128)(2,1)S(1)}, bf16[16,1,32,128]{3,0,2,1:T(8,128)(2,1)S(1)}, u32[]{:S(2)}, u32[]{:S(2)}) %collective-permute-start.19) | collective-permute-done | bytes 131104 | tf_op jit(solution)/shard_map/ppermute | solution.py:17
  155.1 2.0 collective-permute-start.20
  157.1 1.3 collective-permute-start.21
  158.6 3.0 %collective-permute-done.21 = bf16[16,6,1,128]{3,0,2,1:T(8,128)(2,1)S(1)} collective-permute-done((bf16[16,6,1,128]{3,0,2,1:T(8,128)(2,1)S(1)}, bf16[16,6,1,128]{3,0,2,1:T(8,128)(2,1)S(1)}, u32[]{:S(2)}, u32[]{:S(2)}) %collective-permute-start.21) | collective-permute-done | bytes 24608 | tf_op jit(solution)/shard_map/ppermute | solution.py:17
  163.1 2.6 %collective-permute-start.22 = (bf16[16,6,34,1]{2,0,3,1:T(8,128)(2,1)S(1)}, bf16[16,6,34,1]{2,0,3,1:T(8,128)(2,1)S(1)}, u32[]{:S(2)}, u32[]{:S(2)}) collective-permute-start(bf16[16,6,34,1]{2,0,3,1:T(8,128)(2,1)S(1)} %copy.297), channel_id=1, source_target_pairs={{0,1},{2,3},{4,5},{6,7},{8,9},{10,11},{12,13},{14,15},{16,17},{18,... | collective-permute-start | bytes 19592 | tf_op jit(solution)/shard_map/ppermute | solution.py:16
  166.6 1.5 collective-permute-start.23
  169.8 1.3 collective-permute-done.23
  172.0 1.9 pad_maximum_fusion.2
  173.9 1.4 convert_bitcast_fusion
  175.3 3.7 %fusion.387 = (bf16[3,16,4,32,128]{4,3,2,1,0:T(8,128)(2,1)S(1)}, bf16[3,16,4,32,128]{4,3,2,1,0:T(8,128)(2,1)S(1)}, bf16[3,16,4,32,128]{4,3,2,1,0:T(8,128)(2,1)S(...) fusion(bf16[3,16,6,34,128]{4,3,2,1,0:T(8,128)(2,1)S(1)} %conver, ...), kind=kLoop, calls=%fused_computation.258 | loop fusion | bytes 28311552 | tf_op jit(solution)/shard_map/slice | solution.py:50
  187.4 1.1 fusion.326
  188.6 17.0 %all_to_all.12 = bf16[2,1,16,4,32,128]{5,2,4,3,1,0:T(8,128)(2,1)S(1)} all-to-all(bf16[2,1,16,4,32,128]{5,2,4,3,1,0:T(8,128)(2,1)S(1)} %pad_maximum_fusion.3), channel_id=1, replica_groups=mesh['segment'=2,'gx'=8,'gy'=4,'gz'=2] {'segment'}, dimensions={0} | all-to-all | bytes 2097152 | tf_op jit(solution)/shard_map/all_to_all | solution.py:74
  205.6 1.2 copy.319
  (130 shorter events, 46.3 us)
Async XLA Ops:
  0.0 1.2 copy-start
  0.0 8.7 %copy-start.2 = (bf16[1,2,16,16,3,3,3]{3,2,6,5,4,1,0:T(8,128)(2,1)S(1)}, bf16[1,2,16,16,3,3,3]{3,2,6,5,4,1,0:T(8,128)(2,1)}, u32[]{:S(2)}) copy-start(bf16[1,2,16,16,3,3,3]{3,2,6,5,4,1,0:T(8,128)(2,1)} %param.4) | copy-start | bytes 82948
  0.0 9.0 %copy-start.3 = (bf16[1,2,16]{2,1,0:T(2,128)(2,1)S(1)}, bf16[1,2,16]{2,1,0:T(2,128)(2,1)}, u32[]{:S(2)}) copy-start(bf16[1,2,16]{2,1,0:T(2,128)(2,1)} %param.5) | copy-start | bytes 196
  1.3 10.5 %collective-permute-start = (bf16[16,1,32,128]{3,2,1,0:T(8,128)(2,1)S(1)}, bf16[16,1,32,128]{3,2,1,0:T(8,128)(2,1)S(1)}, u32[]{:S(2)}, u32[]{:S(2)}) collective-permute-start(bf16[16,1,32,128]{3,2,1,0:T(8,128)(2,1)S(1)} %get-tuple-element.67), channel_id=1, source_target_pairs={{0,8},{8,16},{16,24},{24,32},{32,40},{40,48},{48,56},{1,9},{9,17},... | collective-permute-start | bytes 393224 | tf_op jit(solution)/shard_map/ppermute | solution.py:16
  6.7 9.3 %collective-permute-start.1 = (bf16[16,1,32,128]{3,2,1,0:T(8,128)(2,1)S(1)}, bf16[16,1,32,128]{3,2,1,0:T(8,128)(2,1)S(1)}, u32[]{:S(2)}, u32[]{:S(2)}) collective-permute-start(bf16[16,1,32,128]{3,2,1,0:T(8,128)(2,1)S(1)} %get-tuple-element.68), channel_id=1, source_target_pairs={{8,0},{16,8},{24,16},{32,24},{40,32},{48,40},{56,48},{9,1},{17,9},... | collective-permute-start | bytes 393224 | tf_op jit(solution)/shard_map/ppermute | solution.py:17
  16.1 4.6 %collective-permute-start.2 = (bf16[16,6,1,128]{3,2,1,0:T(2,128)(2,1)S(1)}, bf16[16,6,1,128]{3,2,1,0:T(2,128)(2,1)S(1)}, u32[]{:S(2)}, u32[]{:S(2)}) collective-permute-start(bf16[16,6,1,128]{3,2,1,0:T(2,128)(2,1)S(1)} %get-tuple-element.59), channel_id=1, source_target_pairs={{0,2},{2,4},{4,6},{1,3},{3,5},{5,7},{8,10},{10,12},{12,14},{9,11},... | collective-permute-start | bytes 73736 | tf_op jit(solution)/shard_map/ppermute | solution.py:16
  19.3 4.8 %collective-permute-start.3 = (bf16[16,6,1,128]{3,2,1,0:T(2,128)(2,1)S(1)}, bf16[16,6,1,128]{3,2,1,0:T(2,128)(2,1)S(1)}, u32[]{:S(2)}, u32[]{:S(2)}) collective-permute-start(bf16[16,6,1,128]{3,2,1,0:T(2,128)(2,1)S(1)} %get-tuple-element.60), channel_id=1, source_target_pairs={{2,0},{4,2},{6,4},{3,1},{5,3},{7,5},{10,8},{12,10},{14,12},{11,9},... | collective-permute-start | bytes 73736 | tf_op jit(solution)/shard_map/ppermute | solution.py:17
  25.8 5.7 %collective-permute-start.4 = (bf16[16,6,34,1]{2,0,3,1:T(8,128)(2,1)S(1)}, bf16[16,6,34,1]{2,0,3,1:T(8,128)(2,1)S(1)}, u32[]{:S(2)}, u32[]{:S(2)}) collective-permute-start(bf16[16,6,34,1]{2,0,3,1:T(8,128)(2,1)S(1)} %copy.228), channel_id=1, source_target_pairs={{0,1},{2,3},{4,5},{6,7},{8,9},{10,11},{12,13},{14,15},{16,17},{18,... | collective-permute-start | bytes 19592 | tf_op jit(solution)/shard_map/ppermute | solution.py:16
  29.1 4.6 %collective-permute-start.5 = (bf16[16,6,34,1]{2,0,3,1:T(8,128)(2,1)S(1)}, bf16[16,6,34,1]{2,0,3,1:T(8,128)(2,1)S(1)}, u32[]{:S(2)}, u32[]{:S(2)}) collective-permute-start(bf16[16,6,34,1]{2,0,3,1:T(8,128)(2,1)S(1)} %copy.229), channel_id=1, source_target_pairs={{1,0},{3,2},{5,4},{7,6},{9,8},{11,10},{13,12},{15,14},{17,16},{19,... | collective-permute-start | bytes 19592 | tf_op jit(solution)/shard_map/ppermute | solution.py:17
  50.7 5.7 %collective-permute-start.6 = (bf16[16,1,32,128]{3,0,2,1:T(8,128)(2,1)S(1)}, bf16[16,1,32,128]{3,0,2,1:T(8,128)(2,1)S(1)}, u32[]{:S(2)}, u32[]{:S(2)}) collective-permute-start(bf16[16,1,32,128]{3,0,2,1:T(8,128)(2,1)S(1)} %get-tuple-element.65), channel_id=1, source_target_pairs={{0,8},{8,16},{16,24},{24,32},{32,40},{40,48},{48,56},{1,9},{9,17},... | collective-permute-start | bytes 393224 | tf_op jit(solution)/shard_map/ppermute | solution.py:16
  54.4 9.3 %collective-permute-start.7 = (bf16[16,1,32,128]{3,0,2,1:T(8,128)(2,1)S(1)}, bf16[16,1,32,128]{3,0,2,1:T(8,128)(2,1)S(1)}, u32[]{:S(2)}, u32[]{:S(2)}) collective-permute-start(bf16[16,1,32,128]{3,0,2,1:T(8,128)(2,1)S(1)} %get-tuple-element.66), channel_id=1, source_target_pairs={{8,0},{16,8},{24,16},{32,24},{40,32},{48,40},{56,48},{9,1},{17,9},... | collective-permute-start | bytes 393224 | tf_op jit(solution)/shard_map/ppermute | solution.py:17
  63.8 5.0 %collective-permute-start.8 = (bf16[16,6,1,128]{3,0,2,1:T(8,128)(2,1)S(1)}, bf16[16,6,1,128]{3,0,2,1:T(8,128)(2,1)S(1)}, u32[]{:S(2)}, u32[]{:S(2)}) collective-permute-start(bf16[16,6,1,128]{3,0,2,1:T(8,128)(2,1)S(1)} %get-tuple-element.57), channel_id=1, source_target_pairs={{0,2},{2,4},{4,6},{1,3},{3,5},{5,7},{8,10},{10,12},{12,14},{9,11},... | collective-permute-start | bytes 73736 | tf_op jit(solution)/shard_map/ppermute | solution.py:16
  67.0 4.6 %collective-permute-start.9 = (bf16[16,6,1,128]{3,0,2,1:T(8,128)(2,1)S(1)}, bf16[16,6,1,128]{3,0,2,1:T(8,128)(2,1)S(1)}, u32[]{:S(2)}, u32[]{:S(2)}) collective-permute-start(bf16[16,6,1,128]{3,0,2,1:T(8,128)(2,1)S(1)} %get-tuple-element.58), channel_id=1, source_target_pairs={{2,0},{4,2},{6,4},{3,1},{5,3},{7,5},{10,8},{12,10},{14,12},{11,9},... | collective-permute-start | bytes 73736 | tf_op jit(solution)/shard_map/ppermute | solution.py:17
  73.0 5.0 %collective-permute-start.10 = (bf16[16,6,34,1]{2,0,3,1:T(8,128)(2,1)S(1)}, bf16[16,6,34,1]{2,0,3,1:T(8,128)(2,1)S(1)}, u32[]{:S(2)}, u32[]{:S(2)}) collective-permute-start(bf16[16,6,34,1]{2,0,3,1:T(8,128)(2,1)S(1)} %copy.249), channel_id=1, source_target_pairs={{0,1},{2,3},{4,5},{6,7},{8,9},{10,11},{12,13},{14,15},{16,17},{18,... | collective-permute-start | bytes 19592 | tf_op jit(solution)/shard_map/ppermute | solution.py:16
  75.7 4.6 %collective-permute-start.11 = (bf16[16,6,34,1]{2,0,3,1:T(8,128)(2,1)S(1)}, bf16[16,6,34,1]{2,0,3,1:T(8,128)(2,1)S(1)}, u32[]{:S(2)}, u32[]{:S(2)}) collective-permute-start(bf16[16,6,34,1]{2,0,3,1:T(8,128)(2,1)S(1)} %copy.250), channel_id=1, source_target_pairs={{1,0},{3,2},{5,4},{7,6},{9,8},{11,10},{13,12},{15,14},{17,16},{19,... | collective-permute-start | bytes 19592 | tf_op jit(solution)/shard_map/ppermute | solution.py:17
  98.1 5.7 %collective-permute-start.12 = (bf16[16,1,32,128]{3,0,2,1:T(8,128)(2,1)S(1)}, bf16[16,1,32,128]{3,0,2,1:T(8,128)(2,1)S(1)}, u32[]{:S(2)}, u32[]{:S(2)}) collective-permute-start(bf16[16,1,32,128]{3,0,2,1:T(8,128)(2,1)S(1)} %get-tuple-element.63), channel_id=1, source_target_pairs={{0,8},{8,16},{16,24},{24,32},{32,40},{40,48},{48,56},{1,9},{9,17},... | collective-permute-start | bytes 393224 | tf_op jit(solution)/shard_map/ppermute | solution.py:16
  100.3 9.3 %collective-permute-start.13 = (bf16[16,1,32,128]{3,0,2,1:T(8,128)(2,1)S(1)}, bf16[16,1,32,128]{3,0,2,1:T(8,128)(2,1)S(1)}, u32[]{:S(2)}, u32[]{:S(2)}) collective-permute-start(bf16[16,1,32,128]{3,0,2,1:T(8,128)(2,1)S(1)} %get-tuple-element.64), channel_id=1, source_target_pairs={{8,0},{16,8},{24,16},{32,24},{40,32},{48,40},{56,48},{9,1},{17,9},... | collective-permute-start | bytes 393224 | tf_op jit(solution)/shard_map/ppermute | solution.py:17
  109.6 4.4 %collective-permute-start.14 = (bf16[16,6,1,128]{3,0,2,1:T(8,128)(2,1)S(1)}, bf16[16,6,1,128]{3,0,2,1:T(8,128)(2,1)S(1)}, u32[]{:S(2)}, u32[]{:S(2)}) collective-permute-start(bf16[16,6,1,128]{3,0,2,1:T(8,128)(2,1)S(1)} %get-tuple-element.55), channel_id=1, source_target_pairs={{0,2},{2,4},{4,6},{1,3},{3,5},{5,7},{8,10},{10,12},{12,14},{9,11},... | collective-permute-start | bytes 73736 | tf_op jit(solution)/shard_map/ppermute | solution.py:16
  112.5 4.8 %collective-permute-start.15 = (bf16[16,6,1,128]{3,0,2,1:T(8,128)(2,1)S(1)}, bf16[16,6,1,128]{3,0,2,1:T(8,128)(2,1)S(1)}, u32[]{:S(2)}, u32[]{:S(2)}) collective-permute-start(bf16[16,6,1,128]{3,0,2,1:T(8,128)(2,1)S(1)} %get-tuple-element.56), channel_id=1, source_target_pairs={{2,0},{4,2},{6,4},{3,1},{5,3},{7,5},{10,8},{12,10},{14,12},{11,9},... | collective-permute-start | bytes 73736 | tf_op jit(solution)/shard_map/ppermute | solution.py:17
  118.7 5.3 %collective-permute-start.16 = (bf16[16,6,34,1]{2,0,3,1:T(8,128)(2,1)S(1)}, bf16[16,6,34,1]{2,0,3,1:T(8,128)(2,1)S(1)}, u32[]{:S(2)}, u32[]{:S(2)}) collective-permute-start(bf16[16,6,34,1]{2,0,3,1:T(8,128)(2,1)S(1)} %copy.275), channel_id=1, source_target_pairs={{0,1},{2,3},{4,5},{6,7},{8,9},{10,11},{12,13},{14,15},{16,17},{18,... | collective-permute-start | bytes 19592 | tf_op jit(solution)/shard_map/ppermute | solution.py:16
  121.7 4.6 %collective-permute-start.17 = (bf16[16,6,34,1]{2,0,3,1:T(8,128)(2,1)S(1)}, bf16[16,6,34,1]{2,0,3,1:T(8,128)(2,1)S(1)}, u32[]{:S(2)}, u32[]{:S(2)}) collective-permute-start(bf16[16,6,34,1]{2,0,3,1:T(8,128)(2,1)S(1)} %copy.276), channel_id=1, source_target_pairs={{1,0},{3,2},{5,4},{7,6},{9,8},{11,10},{13,12},{15,14},{17,16},{19,... | collective-permute-start | bytes 19592 | tf_op jit(solution)/shard_map/ppermute | solution.py:17
  143.6 5.7 %collective-permute-start.18 = (bf16[16,1,32,128]{3,0,2,1:T(8,128)(2,1)S(1)}, bf16[16,1,32,128]{3,0,2,1:T(8,128)(2,1)S(1)}, u32[]{:S(2)}, u32[]{:S(2)}) collective-permute-start(bf16[16,1,32,128]{3,0,2,1:T(8,128)(2,1)S(1)} %get-tuple-element.61), channel_id=1, source_target_pairs={{0,8},{8,16},{16,24},{24,32},{32,40},{40,48},{48,56},{1,9},{9,17},... | collective-permute-start | bytes 393224 | tf_op jit(solution)/shard_map/ppermute | solution.py:16
  145.7 9.3 %collective-permute-start.19 = (bf16[16,1,32,128]{3,0,2,1:T(8,128)(2,1)S(1)}, bf16[16,1,32,128]{3,0,2,1:T(8,128)(2,1)S(1)}, u32[]{:S(2)}, u32[]{:S(2)}) collective-permute-start(bf16[16,1,32,128]{3,0,2,1:T(8,128)(2,1)S(1)} %get-tuple-element.62), channel_id=1, source_target_pairs={{8,0},{16,8},{24,16},{32,24},{40,32},{48,40},{56,48},{9,1},{17,9},... | collective-permute-start | bytes 393224 | tf_op jit(solution)/shard_map/ppermute | solution.py:17
  155.1 3.6 %collective-permute-start.20 = (bf16[16,6,1,128]{3,0,2,1:T(8,128)(2,1)S(1)}, bf16[16,6,1,128]{3,0,2,1:T(8,128)(2,1)S(1)}, u32[]{:S(2)}, u32[]{:S(2)}) collective-permute-start(bf16[16,6,1,128]{3,0,2,1:T(8,128)(2,1)S(1)} %get-tuple-element.53), channel_id=1, source_target_pairs={{0,2},{2,4},{4,6},{1,3},{3,5},{5,7},{8,10},{10,12},{12,14},{9,11},... | collective-permute-start | bytes 73736 | tf_op jit(solution)/shard_map/ppermute | solution.py:16
  157.1 4.6 %collective-permute-start.21 = (bf16[16,6,1,128]{3,0,2,1:T(8,128)(2,1)S(1)}, bf16[16,6,1,128]{3,0,2,1:T(8,128)(2,1)S(1)}, u32[]{:S(2)}, u32[]{:S(2)}) collective-permute-start(bf16[16,6,1,128]{3,0,2,1:T(8,128)(2,1)S(1)} %get-tuple-element.54), channel_id=1, source_target_pairs={{2,0},{4,2},{6,4},{3,1},{5,3},{7,5},{10,8},{12,10},{14,12},{11,9},... | collective-permute-start | bytes 73736 | tf_op jit(solution)/shard_map/ppermute | solution.py:17
  163.1 5.9 %collective-permute-start.22 = (bf16[16,6,34,1]{2,0,3,1:T(8,128)(2,1)S(1)}, bf16[16,6,34,1]{2,0,3,1:T(8,128)(2,1)S(1)}, u32[]{:S(2)}, u32[]{:S(2)}) collective-permute-start(bf16[16,6,34,1]{2,0,3,1:T(8,128)(2,1)S(1)} %copy.297), channel_id=1, source_target_pairs={{0,1},{2,3},{4,5},{6,7},{8,9},{10,11},{12,13},{14,15},{16,17},{18,... | collective-permute-start | bytes 19592 | tf_op jit(solution)/shard_map/ppermute | solution.py:16
  166.6 4.6 %collective-permute-start.23 = (bf16[16,6,34,1]{2,0,3,1:T(8,128)(2,1)S(1)}, bf16[16,6,34,1]{2,0,3,1:T(8,128)(2,1)S(1)}, u32[]{:S(2)}, u32[]{:S(2)}) collective-permute-start(bf16[16,6,34,1]{2,0,3,1:T(8,128)(2,1)S(1)} %copy.298), channel_id=1, source_target_pairs={{1,0},{3,2},{5,4},{7,6},{9,8},{11,10},{13,12},{15,14},{17,16},{19,... | collective-permute-start | bytes 19592 | tf_op jit(solution)/shard_map/ppermute | solution.py:17
  188.6 18.3 %copy-start.1 = (bf16[2,16,4,32,128]{4,3,2,1,0:T(8,128)(2,1)S(1)}, bf16[2,16,4,32,128]{4,3,2,1,0:T(8,128)(2,1)}, u32[]{:S(2)}) copy-start(bf16[2,16,4,32,128]{4,3,2,1,0:T(8,128)(2,1)} %param.3) | copy-start | bytes 3145732
where the time goes:
time: 211 us; the launch traced here: 207 us
  starting transfers between devices  55 us (26%)
  matrix products  45.5 us (22%)
  waiting for transfers between devices  42.2 us (20%)
  local copies, waits for them, and re-layouts  37 us (18%)
  blocking collectives  19.5 us (9%)
  other arithmetic  7.18 us (3%)
    ppermute x12, waiting for transfers between devices, with_halo(): after = lax.ppermute(initial, axis, down)  41.2 us
    dot_general x36, matrix products, convolve(): jnp.einsum('oid,dixyz->oxyz', taps, slab, preferred_element_type=jnp.floa...  38.4 us
    ppermute x12, starting transfers between devices, with_halo(): before = lax.ppermute(last, axis, up)  33.9 us
    ppermute x12, starting transfers between devices, with_halo(): after = lax.ppermute(initial, axis, down)  21.1 us
    all_to_all x1, blocking collectives, shards(): lax.all_to_all(stacked, 'segment', split_axis=0, concat_axis=1, tiled=True)  17 us
    slice x4, local copies, waits for them, and re-layouts, convolve(): slab = shifted[:, :, step_x:step_x + depth, step_y:step_y + height, :]  15 us
    dot_general x4, matrix products, convolve(): jnp.einsum('cxyw,wdz->dcxyz', padded, band_table(width), preferred_elemen...  7.05 us
    concatenate x7, other arithmetic, with_halo(): value = jnp.concatenate([before, value, after], axis=dim)  6.71 us
  transfers between devices with their start and end apart: 24, of which 15 were waited for; matrix products, arithmetic and copies ran while one was open for 6% of the time, Pallas kernels for 0%

commit v1 on v0

v1 whole, which is shorter than its diff:
```python
import functools

import jax
import jax.numpy as jnp
from jax import lax
from jax.experimental import pallas as pl
from jax.experimental.pallas import tpu as pltpu
from jax.sharding import PartitionSpec as P

MESH = pl.DeviceIdType.MESH
BF = jnp.bfloat16
F32 = jnp.float32

NXL, NYL, C, L = 4, 32, 16, 128
FX, FY = NXL + 4, NYL + 6
HX, HY = NXL + 2, NYL + 4
KT = 1280


def dots(a, b):
    return jnp.dot(a, b, preferred_element_type=F32)


def leaky(v):
    return jnp.maximum(v, 0.2 * v)


def kernel(
    sizes, feat, wts, bias, out,
    raw, wall, ball, f1, f2, fm, fp, h0, hm, hp, tm, ws, base, brow, wbase, pm, ones,
    eb1, eb2, yb1, yb2, hn, res, stage,
    lsem, wsem, wrs, ssx, rsx, ssy, rsy, ssz, rsz, sso, rso,
):
    ngx, ngy = sizes
    seg, gx = lax.axis_index("segment"), lax.axis_index("gx")
    gy, gz = lax.axis_index("gy"), lax.axis_index("gz")
    has = {
        ("x", 1): gx < ngx - 1, ("x", -1): gx > 0,
        ("y", 1): gy < ngy - 1, ("y", -1): gy > 0,
    }
    here = {"x": gx, "y": gy}

    def to(axis, step):
        return {"g" + axis: here[axis] + step}

    load = pltpu.make_async_copy(feat.at[seg], raw, lsem.at[0])
    load.start()
    wl = pltpu.make_async_copy(wts, wall.at[seg], lsem.at[1])
    wl.start()
    bl = pltpu.make_async_copy(bias, ball.at[seg], lsem.at[2])
    bl.start()

    zrow = jnp.zeros((C, L), BF)

    def clear(ref, x0, x1, y0, y1):
        def body(i, c):
            for y in range(y0, y1):
                ref[i, y] = zrow
            return c
        lax.fori_loop(x0, x1, body, 0)

    for f in (f1, f2):
        clear(f, 0, FX, NYL + 4, FY)
        pl.when(gx == 0)(lambda f=f: clear(f, 0, 2, 0, FY))
        pl.when(gx == ngx - 1)(lambda f=f: clear(f, FX - 2, FX, 0, FY))
        pl.when(gy == 0)(lambda f=f: clear(f, 0, FX, 0, 2))
        pl.when(gy == ngy - 1)(lambda f=f: clear(f, 0, FX, NYL + 2, NYL + 4))
    for e in (eb1, eb2):
        for s in range(2):
            for i in range(FX):
                e[s, i] = zrow
    for e in (yb1, yb2):
        for d in range(2):
            for s in range(2):
                for i in range(NXL):
                    e[d, s, i] = zrow

    bar = pltpu.get_barrier_semaphore()
    for (axis, step), ok in has.items():
        @pl.when(ok)
        def _(axis=axis, step=step):
            pl.semaphore_signal(bar, inc=1, device_id=to(axis, step), device_id_type=MESH)
    pl.semaphore_signal(bar, inc=1, device_id={"gz": 1 - gz}, device_id_type=MESH)
    pl.semaphore_signal(bar, inc=1, device_id={"segment": 1 - seg}, device_id_type=MESH)

    r = lax.broadcasted_iota(jnp.int32, (256, 256), 0)
    c = lax.broadcasted_iota(jnp.int32, (256, 256), 1)
    pm[...] = jnp.where((r // 16 == c % 16) & (r % 16 == c // 16), 1.0, 0.0).astype(BF)
    orow = lax.broadcasted_iota(jnp.int32, (L, L), 0)
    ones[...] = jnp.where(orow < C, 1.0, 0.0).astype(BF)
    load.wait()
    for y in range(NYL // 16):
        for x in range(0, NXL, 2):
            ab = [raw[:, x + k, 16 * y:16 * y + 16, :].reshape(256, L) for k in range(2)]
            t = dots(pm[...], jnp.concatenate(ab, axis=1)).astype(BF)
            for k in range(2):
                f1[x + k + 2, pl.ds(2 + 16 * y, 16)] = t[:, L * k:L * k + L].reshape(16, C, L)

    count = 2 + sum(jnp.where(ok, 1, 0) for ok in has.values())
    pl.semaphore_wait(bar, count)

    def xcopy(q, f, eb, step, k):
        d = 0 if step > 0 else 1
        mv = -NXL * step
        near, far = (FX - 3, FX - 4) if step > 0 else (2, 3)
        lo = FX - 4 if step > 0 else 2
        part = (
            lambda o: f.at[near + o, pl.ds(2, NYL)],
            lambda o: f.at[far + o, pl.ds(2, NYL)],
            lambda o: f.at[pl.ds(lo + o, 2), pl.ds(0, 2)],
            lambda o: f.at[pl.ds(lo + o, 2), pl.ds(NYL + 2, 2)],
            lambda o: eb.at[:, pl.ds(lo + o, 2)],
        )[k]
        return pltpu.make_async_remote_copy(
            part(0), part(mv), ssx.at[q, d, k], rsx.at[q, d, k],
            device_id=to("x", step), device_id_type=MESH)

    def yrows(q, f, step):
        d = 0 if step > 0 else 1
        src, dst = (NYL, 0) if step > 0 else (2, NYL + 2)
        return pltpu.make_async_remote_copy(
            f.at[pl.ds(2, NXL), pl.ds(src, 2)], f.at[pl.ds(2, NXL), pl.ds(dst, 2)],
            ssy.at[q, d, 0], rsy.at[q, d, 0], device_id=to("y", step), device_id_type=MESH)

    def yedges(q, eb, yb, step):
        d = 0 if step > 0 else 1
        return pltpu.make_async_remote_copy(
            eb.at[:, pl.ds(2, NXL)], yb.at[d],
            ssy.at[q, d, 1], rsy.at[q, d, 1], device_id=to("y", step), device_id_type=MESH)

    def zcopy(q, eb):
        return pltpu.make_async_remote_copy(
            eb.at[0, pl.ds(2, NXL)], eb.at[1, pl.ds(2, NXL)], ssz.at[q], rsz.at[q],
            device_id={"gz": 1 - gz}, device_id_type=MESH)

    def ocopy(q):
        return pltpu.make_async_remote_copy(
            stage.at[q], out.at[seg], sso.at[q], rso.at[q],
            device_id={"segment": 1 - seg}, device_id_type=MESH)

    def lcopy(q):
        return pltpu.make_async_copy(stage.at[q], out.at[seg], lsem.at[3 + q])

    def wcopy(k, ref, sec=seg):
        return pltpu.make_async_remote_copy(
            ref.at[sec], ref.at[sec], wsem.at[k], wrs.at[k],
            device_id={"segment": 1 - seg}, device_id_type=MESH)

    lanes = lax.broadcasted_iota(jnp.int32, (C, L), 1)
    edge = jnp.where(gz == 0, L - 1, 0)
    inner = jnp.where(gz == 0, L - 2, 1)

    def pack_edges(f, eb):
        def plane(x, carry):
            def row(y, acc):
                v = f[x, y]
                a = pltpu.roll(v, lax.rem(y + L - edge, L), 1)
                b = pltpu.roll(v, lax.rem(y + 64 + L - inner, L), 1)
                acc = jnp.where(lanes == y, a, acc)
                return jnp.where(lanes == y + 64, b, acc)
            eb[0, x] = lax.fori_loop(2, NYL + 2, row, zrow, unroll=8)
            return carry
        lax.fori_loop(2, NXL + 2, plane, 0)

    def start_exchange(q, f, eb, yb):
        for step in (1, -1):
            @pl.when(has["x", step])
            def _(step=step):
                xcopy(q, f, eb, step, 0).start()
                xcopy(q, f, eb, step, 1).start()
        for step in (1, -1):
            @pl.when(has["y", step])
            def _(step=step):
                yrows(q, f, step).start()
        pack_edges(f, eb)
        zcopy(q, eb).start()

    def middle_exchange(q, f, eb, yb):
        for step in (1, -1):
            @pl.when(has["y", -step])
            def _(step=step):
                yrows(q, f, step).wait_recv()
        for step in (1, -1):
            @pl.when(has["x", step])
            def _(step=step):
                xcopy(q, f, eb, step, 2).start()
                xcopy(q, f, eb, step, 3).start()
        zcopy(q, eb).wait_recv()
        zcopy(q, eb).wait_send()
        for step in (1, -1):
            @pl.when(has["y", step])
            def _(step=step):
                yedges(q, eb, yb, step).start()
        for step in (1, -1):
            @pl.when(has["y", -step])
            def _(step=step):
                yedges(q, eb, yb, step).wait_recv()
            @pl.when(has["y", step])
            def _(step=step):
                yedges(q, eb, yb, step).wait_send()
        low = lanes % 64
        for s in range(2):
            for x in range(NXL):
                v = eb[s, x + 2]
                v = jnp.where(low < 2, pltpu.roll(yb[0, s, x], L - NYL, 1), v)
                v = jnp.where((low >= NYL + 2) & (low < NYL + 4), pltpu.roll(yb[1, s, x], NYL, 1), v)
                eb[s, x + 2] = v
        for step in (1, -1):
            @pl.when(has["x", step])
            def _(step=step):
                xcopy(q, f, eb, step, 4).start()

    def end_exchange(q, f, eb, yb):
        for step in (1, -1):
            @pl.when(has["x", -step])
            def _(step=step):
                for k in range(5):
                    xcopy(q, f, eb, step, k).wait_recv()
            @pl.when(has["x", step])
            def _(step=step):
                for k in range(5):
                    xcopy(q, f, eb, step, k).wait_send()
            @pl.when(has["y", step])
            def _(step=step):
                yrows(q, f, step).wait_send()

    def make_weights(sec):
        for lay in range(2):
            base[...] = jnp.zeros_like(base)
            for dz in range(3):
                for dx in range(3):
                    for dy in range(3):
                        p = 16 * (dx * 6 + dy)
                        base[dz, :, p:p + 16] = wall[sec, lay, dx * 9 + dy * 3 + dz].astype(F32)
            brow[0:1, 0:C] = ball[sec, lay:lay + 1, :].astype(F32)
            for xq in range(2):
                for yq in range(4):
                    rows = slice(16 * (4 * xq + yq), 16 * (4 * xq + yq) + 16)
                    for dz in range(3):
                        v = base[dz]
                        if 6 * xq + yq:
                            v = pltpu.roll(v, 16 * (6 * xq + yq), 1)
                        tm[2 * sec + lay, rows, 384 * dz:384 * dz + 384] = v.astype(BF)
            br = jnp.broadcast_to(brow[0:1, :], (L, L))
            rr = lax.broadcasted_iota(jnp.int32, (L, L), 0)
            cc = lax.broadcasted_iota(jnp.int32, (L, L), 1)
            diag = jnp.where(rr % 16 == cc, br, 0.0).astype(BF)
            tm[2 * sec + lay, :, 1152:1280] = diag
            if lay == 0:
                wbase[...] = jnp.zeros_like(wbase)
                for dy in range(3):
                    for dx in range(3):
                        for col in range(3):
                            p = 16 * (dx * 3 + col)
                            dz = jnp.where(gz == 0, col, 2 - col)
                            wbase[16 * dy:16 * dy + 16, p:p + 16] = wall[
                                sec, 0, dx * 9 + dy * 3 + dz].astype(F32)
                wbase[16:32, 144:160] = diag[0:16, 0:16].astype(F32)
                ws[sec] = wbase[...].astype(BF)

    def shift_rows(f, eb):
        def plane(x, carry):
            n = eb[1, x]
            def row(y, cc):
                v = f[x, y]
                h = pltpu.roll(n, lax.rem(edge + L - y, L), 1)
                h = jnp.where(lanes == edge, h, zrow)
                fm[x, y] = jnp.where(lanes == 0, h, pltpu.roll(v, 1, 1))
                fp[x, y] = jnp.where(lanes == L - 1, h, pltpu.roll(v, L - 1, 1))
                return cc
            lax.fori_loop(0, NYL + 4, row, 0, unroll=6)
            for y in range(NYL + 4, FY):
                fm[x, y] = zrow
                fp[x, y] = zrow
            return carry
        lax.fori_loop(0, FX, plane, 0)

    def strips(sec, eb):
        one = ones[0:C, :]
        tail = jnp.zeros((256 - 160, L), BF)
        lane = lax.broadcasted_iota(jnp.int32, (C, L), 1)
        for j in range(HX):
            rows = []
            for dx in range(3):
                rows += [eb[0, j + dx], eb[1, j + dx], pltpu.roll(eb[1, j + dx], 64, 1)]
            m = dots(ws[sec], jnp.concatenate(rows + [one, tail], axis=0))
            v = pltpu.roll(m[0:16], 1, 1) + m[16:32] + pltpu.roll(m[32:48], L - 1, 1)
            v = leaky(v)
            bad = (lane == 1) & (gy == 0) | (lane == NYL + 2) & (gy == ngy - 1)
            if j == 0:
                bad = bad | (gx == 0)
            if j == HX - 1:
                bad = bad | (gx == ngx - 1)
            hn[j] = jnp.where(bad, 0.0, v).astype(BF)

    def boxes(lay, fields, pairs):
        cols = []
        for x0, y0 in pairs:
            rows = []
            for f in fields:
                for xr in range(4):
                    rows.append(f[x0 + xr, pl.ds(y0, 6)].reshape(96, L))
            cols.append(jnp.concatenate(rows + [ones[...]], axis=0))
        return dots(tm[lay], jnp.concatenate(cols, axis=1))

    def layer_a(sec, f):
        def body(yt, carry):
            y0 = 4 * yt
            pairs = [(0, y0), (2, y0), (4, y0)]
            v = leaky(boxes(2 * sec, (fm, f, fp), pairs)).astype(BF)
            for k, (x0, _) in enumerate(pairs):
                b = v[:, L * k:L * k + L].reshape(2, 4, C, L)
                for xq in range(2):
                    n = hn[x0 + xq]
                    for yq in range(4):
                        t = b[xq, yq]
                        h = pltpu.roll(n, lax.rem(edge + 2 * L - 1 - y0 - yq, L), 1)
                        h = jnp.where(lanes == edge, h, zrow)
                        h0[x0 + xq, y0 + yq] = t
                        hm[x0 + xq, y0 + yq] = jnp.where(lanes == 0, h, pltpu.roll(t, 1, 1))
                        hp[x0 + xq, y0 + yq] = jnp.where(lanes == L - 1, h, pltpu.roll(t, L - 1, 1))
            return carry
        lax.fori_loop(0, HY // 4, body, 0)
        for ref in (h0, hm, hp):
            pl.when(gx == 0)(lambda ref=ref: clear(ref, 0, 1, 0, HY))
            pl.when(gx == ngx - 1)(lambda ref=ref: clear(ref, HX - 1, HX, 0, HY))
            pl.when(gy == 0)(lambda ref=ref: clear(ref, 0, HX, 0, 1))
            pl.when(gy == ngy - 1)(lambda ref=ref: clear(ref, 0, HX, NYL + 1, NYL + 2))

    def layer_b(sec, g, gx0, gy0):
        def body(yt, carry):
            y0 = 4 * yt
            pairs = [(0, y0), (2, y0)]
            v = leaky(boxes(2 * sec + 1, (hm, h0, hp), pairs)).astype(BF)
            for k, (x0, _) in enumerate(pairs):
                b = v[:, L * k:L * k + L].reshape(2, 4, C, L)
                for xq in range(2):
                    g[gx0 + x0 + xq, pl.ds(gy0 + y0, 4)] = b[xq]
            return carry
        lax.fori_loop(0, NYL // 4, body, 0)

    def to_stage(q, g, gx0, gy0):
        for y in range(NYL // 16):
            for x in range(0, NXL, 2):
                ab = [g[gx0 + x + k, pl.ds(gy0 + 16 * y, 16)].reshape(256, L) for k in range(2)]
                t = dots(pm[...], jnp.concatenate(ab, axis=1)).astype(BF)
                for k in range(2):
                    stage[q, :, x + k, 16 * y:16 * y + 16, :] = t[:, L * k:L * k + L].reshape(C, 16, L)

    def send_out(q):
        @pl.when(seg == q)
        def _():
            lcopy(q).start()
        @pl.when(seg != q)
        def _():
            ocopy(q).start()

    start_exchange(0, f1, eb1, yb1)
    wl.wait()
    bl.wait()
    wcopy(0, wall).start()
    wcopy(1, ball).start()
    middle_exchange(0, f1, eb1, yb1)
    brow[...] = jnp.zeros_like(brow)
    wcopy(0, wall, 1 - seg).wait_recv()
    wcopy(1, ball, 1 - seg).wait_recv()
    wcopy(0, wall).wait_send()
    wcopy(1, ball).wait_send()
    for sec in range(2):
        make_weights(sec)
    end_exchange(0, f1, eb1, yb1)

    shift_rows(f1, eb1)
    strips(0, eb1)
    layer_a(0, f1)
    layer_b(0, f2, 2, 2)

    start_exchange(1, f2, eb2, yb2)
    to_stage(0, f2, 2, 2)
    send_out(0)
    middle_exchange(1, f2, eb2, yb2)
    end_exchange(1, f2, eb2, yb2)

    shift_rows(f2, eb2)
    strips(1, eb2)
    layer_a(1, f2)
    layer_b(1, res, 0, 0)
    to_stage(1, res, 0, 0)
    send_out(1)

    for q in range(2):
        @pl.when(seg == q)
        def _(q=q):
            lcopy(q).wait()
            pltpu.make_async_remote_copy(
                stage.at[q], out.at[1 - seg], sso.at[q], rso.at[q],
                device_id={"segment": 1 - seg}, device_id_type=MESH).wait_recv()
        @pl.when(seg != q)
        def _(q=q):
            ocopy(q).wait_send()


def shards(sizes, features, weights, biases):
    w = weights[0].transpose(0, 3, 4, 5, 1, 2).reshape(2, 27, C, C)
    any_space = pl.BlockSpec(memory_space=pl.ANY)
    dma = pltpu.SemaphoreType.DMA
    out = pl.pallas_call(
        functools.partial(kernel, sizes),
        name="sections",
        out_shape=jax.ShapeDtypeStruct((2, C, NXL, NYL, L), BF),
        in_specs=[any_space] * 3,
        out_specs=any_space,
        scratch_shapes=[
            pltpu.VMEM((C, NXL, NYL, L), BF),
            pltpu.VMEM((2, 2, 27, C, C), BF),
            pltpu.VMEM((2, 2, C), BF),
            pltpu.VMEM((FX, FY, C, L), BF),
            pltpu.VMEM((FX, FY, C, L), BF),
            pltpu.VMEM((FX, FY, C, L), BF),
            pltpu.VMEM((FX, FY, C, L), BF),
            pltpu.VMEM((HX, HY, C, L), BF),
            pltpu.VMEM((HX, HY, C, L), BF),
            pltpu.VMEM((HX, HY, C, L), BF),
            pltpu.VMEM((4, L, KT), BF),
            pltpu.VMEM((2, 48, 256), BF),
            pltpu.VMEM((3, C, 384), F32),
            pltpu.VMEM((8, L), F32),
            pltpu.VMEM((48, 256), F32),
            pltpu.VMEM((256, 256), BF),
            pltpu.VMEM((L, L), BF),
            pltpu.VMEM((2, FX, C, L), BF),
            pltpu.VMEM((2, FX, C, L), BF),
            pltpu.VMEM((2, 2, NXL, C, L), BF),
            pltpu.VMEM((2, 2, NXL, C, L), BF),
            pltpu.VMEM((HX, C, L), BF),
            pltpu.VMEM((NXL, NYL, C, L), BF),
            pltpu.VMEM((2, C, NXL, NYL, L), BF),
            dma((5,)), dma((2,)), dma((2,)),
            dma((2, 2, 5)), dma((2, 2, 5)),
            dma((2, 2, 2)), dma((2, 2, 2)),
            dma((2,)), dma((2,)), dma((2,)), dma((2,)),
        ],
        compiler_params=pltpu.CompilerParams(
            collective_id=0, has_side_effects=True, vmem_limit_bytes=60 << 20),
    )(features, w, biases[0])
    return out[None]


def solution(mesh):
    placed = (
        P(None, None, "gx", "gy", "gz"),
        P("segment", None, None, None, None, None, None),
        P("segment", None, None),
    )
    sizes = (mesh.shape["gx"], mesh.shape["gy"])
    return jax.shard_map(
        functools.partial(shards, sizes),
        mesh=mesh,
        in_specs=placed,
        out_specs=P("segment", None, None, "gx", "gy", "gz"),
        check_vma=False,
    )
```

time: 211 us -> 56.9 us (0.27); the launches traced: 207 us -> 56.6 us
  starting transfers between devices: 55 us -> 0 us
  Pallas kernels: 0 us -> 54.3 us
  matrix products: 45.5 us -> 0 us
  waiting for transfers between devices: 42.2 us -> 0 us
  local copies, waits for them, and re-layouts: 37 us -> 2.31 us
  blocking collectives: 19.5 us -> 0 us
  other arithmetic: 7.18 us -> 0 us
    ppermute x24 -> x0, starting transfers between devices: 55 us -> none  [the longest x12 33.9 us: with_halo(): before = lax.ppermute(last, axis, up)]
    pallas_call x0 -> x1, Pallas kernels: none -> 54.3 us  [shards(): pl.pallas_call(functools.partial(kernel, sizes), name='sections', out_sha...]
    dot_general x40 -> x0, matrix products: 45.5 us -> none  [the longest x36 38.4 us: convolve(): jnp.einsum('oid,dixyz->oxyz', taps, slab, preferred_element_type=jnp.floa...]
    ppermute x24 -> x0, waiting for transfers between devices: 42.2 us -> none  [the longest x12 41.2 us: with_halo(): after = lax.ppermute(initial, axis, down)]
    slice x29 -> x0, local copies, waits for them, and re-layouts: 23.9 us -> none  [the longest x4 15 us: convolve(): slab = shifted[:, :, step_x:step_x + depth, step_y:step_y + height, :]]
    all_to_all x1 -> x0, blocking collectives: 17 us -> none  [shards(): lax.all_to_all(stacked, 'segment', split_axis=0, concat_axis=1, tiled=True)]
    concatenate x8 -> x0, other arithmetic: 6.79 us -> none  [the longest x7 6.71 us: with_halo(): value = jnp.concatenate([before, value, after], axis=dim)]
    ppermute x8 -> x0, local copies, waits for them, and re-layouts: 6.48 us -> none  [the longest x4 3.25 us: with_halo(): before = lax.ppermute(last, axis, up)]
  transfers between devices with their start and end apart: 24 -> 0, of which waited for: 15 -> 0; matrix products, arithmetic and copies ran while one was open for 6% -> 0% of each run, Pallas kernels for 0% -> 0%
where the time goes in v1:
time: 56.9 us; the launch traced here: 56.6 us
  Pallas kernels  54.3 us (95%)
  local copies, waits for them, and re-layouts  2.31 us (4%)
    pallas_call x1, Pallas kernels, shards(): pl.pallas_call(functools.partial(kernel, sizes), name='sections', out_sha...  54.3 us
    unnamed x1, local copies, waits for them, and re-layouts  2.31 us

profile of v1, /device:TPU:7, one launch (start us, length us, event | category | flops | bytes accessed | tf_op | source)
XLA Modules:
  0.0 56.6 jit_solution(13532097985386858978)
XLA Ops:
  0.0 54.3 %sections.1 = bf16[2,16,4,32,128]{4,3,2,1,0:T(8,128)(2,1)} custom-call(bf16[2,16,4,32,128]{4,3,2,1,0:T(8,128)(2,1)} %feat.1, bf16[2,27,16,16]{3,2,1,0:T(8,128)(2,1)} %bitcast.8, bf16[2,16]{1,0:T(2,128)(2,1)} %bitcast.9), custom_call_target="tpu_custom_call" | custom-call | tf_op jit(solution)/shard_map/sections/pallas_call | solution.py:407
  54.3 2.3 %copy.5 = bf16[1,2,16,4,32,128]{5,4,3,2,1,0:T(8,128)(2,1)} copy(bf16[1,2,16,4,32,128]{5,4,3,2,1,0:T(8,128)(2,1)} %bitcast.7) | data formatting | bytes 2097152

commit v2 on v1

--- a/solution.py
+++ b/solution.py
@@ -21,13 +21,21 @@
     return jnp.dot(a, b, preferred_element_type=F32)
 
 
+def iota(shape, dim):
+    return lax.broadcasted_iota(jnp.int32, shape, dim)
+
+
+def one_hot(hit):
+    return jnp.where(hit, 1.0, 0.0).astype(BF)
+
+
 def leaky(v):
     return jnp.maximum(v, 0.2 * v)
 
 
 def kernel(
     sizes, feat, wts, bias, out,
-    raw, wall, ball, f1, f2, fm, fp, h0, hm, hp, tm, ws, base, brow, wbase, pm, ones,
+    raw, wall, ball, f1, f2, fm, fp, h0, hm, hp, tm, ws, base, brow, wbase, pm, ones, sh, sy, xe,
     eb1, eb2, yb1, yb2, hn, res, stage,
     lsem, wsem, wrs, ssx, rsx, ssy, rsy, ssz, rsz, sso, rso,
 ):
@@ -42,6 +50,10 @@
 
     def to(axis, step):
         return {"g" + axis: here[axis] + step}
+
+    lanes = iota((C, L), 1)
+    edge = jnp.where(gz == 0, L - 1, 0)
+    inner = jnp.where(gz == 0, L - 2, 1)
 
     load = pltpu.make_async_copy(feat.at[seg], raw, lsem.at[0])
     load.start()
@@ -88,6 +100,18 @@
     pm[...] = jnp.where((r // 16 == c % 16) & (r % 16 == c // 16), 1.0, 0.0).astype(BF)
     orow = lax.broadcasted_iota(jnp.int32, (L, L), 0)
     ones[...] = jnp.where(orow < C, 1.0, 0.0).astype(BF)
+    rl, cl = iota((L, 2 * L), 0), iota((L, 2 * L), 1)
+    sh[...] = one_hot((cl < L) & (rl == cl - 1) | (cl >= L) & (rl == cl - L + 1))
+    target = jnp.where(gz == 0, 2 * L - 1, 0)
+    def table_s(i, carry):
+        sy[i] = one_hot((rl == i) & (cl == target))
+        return carry
+    re, ce = iota((L, L), 0), iota((L, L), 1)
+    def table_e(y, carry):
+        hit = (re == edge) & (ce == y + 2) | (re == inner) & (ce == y + 66)
+        xe[pl.ds(pl.multiple_of(L * y, L), L), :] = one_hot(hit)
+        return carry
+    lax.fori_loop(0, NYL, table_e, 0)
     load.wait()
     for y in range(NYL // 16):
         for x in range(0, NXL, 2):
@@ -146,21 +170,14 @@
             ref.at[sec], ref.at[sec], wsem.at[k], wrs.at[k],
             device_id={"segment": 1 - seg}, device_id_type=MESH)
 
-    lanes = lax.broadcasted_iota(jnp.int32, (C, L), 1)
-    edge = jnp.where(gz == 0, L - 1, 0)
-    inner = jnp.where(gz == 0, L - 2, 1)
 
     def pack_edges(f, eb):
-        def plane(x, carry):
-            def row(y, acc):
-                v = f[x, y]
-                a = pltpu.roll(v, lax.rem(y + L - edge, L), 1)
-                b = pltpu.roll(v, lax.rem(y + 64 + L - inner, L), 1)
-                acc = jnp.where(lanes == y, a, acc)
-                return jnp.where(lanes == y + 64, b, acc)
-            eb[0, x] = lax.fori_loop(2, NYL + 2, row, zrow, unroll=8)
-            return carry
-        lax.fori_loop(2, NXL + 2, plane, 0)
+        acc = None
+        for y in range(0, NYL, 2):
+            lhs = [f[pl.ds(2, NXL), 2 + y + k].reshape(NXL * C, L) for k in range(2)]
+            t = dots(jnp.concatenate(lhs, axis=1), xe[pl.ds(L * y, 2 * L), :])
+            acc = t if acc is None else acc + t
+        eb[0, pl.ds(2, NXL)] = acc.astype(BF).reshape(NXL, C, L)
 
     def start_exchange(q, f, eb, yb):
         for step in (1, -1):
@@ -258,22 +275,18 @@
                 wbase[16:32, 144:160] = diag[0:16, 0:16].astype(F32)
                 ws[sec] = wbase[...].astype(BF)
 
-    def shift_rows(f, eb):
-        def plane(x, carry):
-            n = eb[1, x]
-            def row(y, cc):
-                v = f[x, y]
-                h = pltpu.roll(n, lax.rem(edge + L - y, L), 1)
-                h = jnp.where(lanes == edge, h, zrow)
-                fm[x, y] = jnp.where(lanes == 0, h, pltpu.roll(v, 1, 1))
-                fp[x, y] = jnp.where(lanes == L - 1, h, pltpu.roll(v, L - 1, 1))
-                return cc
-            lax.fori_loop(0, NYL + 4, row, 0, unroll=6)
-            for y in range(NYL + 4, FY):
-                fm[x, y] = zrow
-                fp[x, y] = zrow
+    def shift(src, edges, n, first, dm, dp):
+        def body(i, carry):
+            e = edges.reshape(n * C, L)
+            for k in range(4):
+                y = 4 * i + k
+                lhs = jnp.concatenate([src[:, y].reshape(n * C, L), e], axis=1)
+                rhs = jnp.concatenate([sh[...], sy[first + y]], axis=0)
+                t = dots(lhs, rhs).astype(BF)
+                dm[:, y] = t[:, :L].reshape(n, C, L)
+                dp[:, y] = t[:, L:].reshape(n, C, L)
             return carry
-        lax.fori_loop(0, FX, plane, 0)
+        lax.fori_loop(0, HY // 4, body, 0)
 
     def strips(sec, eb):
         one = ones[0:C, :]
@@ -294,50 +307,46 @@
             hn[j] = jnp.where(bad, 0.0, v).astype(BF)
 
     def boxes(lay, fields, pairs):
-        cols = []
-        for x0, y0 in pairs:
-            rows = []
-            for f in fields:
-                for xr in range(4):
-                    rows.append(f[x0 + xr, pl.ds(y0, 6)].reshape(96, L))
-            cols.append(jnp.concatenate(rows + [ones[...]], axis=0))
-        return dots(tm[lay], jnp.concatenate(cols, axis=1))
+        acc = None
+        for k in range(5):
+            cols = []
+            for x0, y0 in pairs:
+                rows = []
+                for p in range(16 * k, min(16 * k + 16, 72)):
+                    g, yr = divmod(p, 6)
+                    rows.append(fields[g // 4][x0 + g % 4, y0 + yr])
+                if k == 4:
+                    rows.append(ones[...])
+                cols.append(jnp.concatenate(rows, axis=0))
+            t = dots(tm[lay, :, 256 * k:256 * k + 256], jnp.concatenate(cols, axis=1))
+            acc = t if acc is None else acc + t
+        return leaky(acc).astype(BF)
+
+    def layer(lay, fields, todo, n, dst, ox, oy):
+        def body(i, carry):
+            pairs = [todo(4 * i + k) for k in range(4)]
+            for h in range(2):
+                v = boxes(lay, fields, pairs[2 * h:2 * h + 2])
+                for k in range(2):
+                    x0, y0 = pairs[2 * h + k]
+                    b = v[:, L * k:L * k + L].reshape(2, 4, C, L)
+                    for xq in range(2):
+                        dst[ox + x0 + xq, pl.ds(oy + y0, 4)] = b[xq]
+            return carry
+        lax.fori_loop(0, (n + 3) // 4, body, 0)
 
     def layer_a(sec, f):
-        def body(yt, carry):
-            y0 = 4 * yt
-            pairs = [(0, y0), (2, y0), (4, y0)]
-            v = leaky(boxes(2 * sec, (fm, f, fp), pairs)).astype(BF)
-            for k, (x0, _) in enumerate(pairs):
-                b = v[:, L * k:L * k + L].reshape(2, 4, C, L)
-                for xq in range(2):
-                    n = hn[x0 + xq]
-                    for yq in range(4):
-                        t = b[xq, yq]
-                        h = pltpu.roll(n, lax.rem(edge + 2 * L - 1 - y0 - yq, L), 1)
-                        h = jnp.where(lanes == edge, h, zrow)
-                        h0[x0 + xq, y0 + yq] = t
-                        hm[x0 + xq, y0 + yq] = jnp.where(lanes == 0, h, pltpu.roll(t, 1, 1))
-                        hp[x0 + xq, y0 + yq] = jnp.where(lanes == L - 1, h, pltpu.roll(t, L - 1, 1))
-            return carry
-        lax.fori_loop(0, HY // 4, body, 0)
-        for ref in (h0, hm, hp):
-            pl.when(gx == 0)(lambda ref=ref: clear(ref, 0, 1, 0, HY))
-            pl.when(gx == ngx - 1)(lambda ref=ref: clear(ref, HX - 1, HX, 0, HY))
-            pl.when(gy == 0)(lambda ref=ref: clear(ref, 0, HX, 0, 1))
-            pl.when(gy == ngy - 1)(lambda ref=ref: clear(ref, 0, HX, NYL + 1, NYL + 2))
+        def todo(j):
+            j = jnp.minimum(j, 26)
+            return 2 * lax.rem(j, 3), 4 * lax.div(j, 3)
+        layer(2 * sec, (fm, f, fp), todo, 27, h0, 0, 0)
+        pl.when(gx == 0)(lambda: clear(h0, 0, 1, 0, HY))
+        pl.when(gx == ngx - 1)(lambda: clear(h0, HX - 1, HX, 0, HY))
+        pl.when(gy == 0)(lambda: clear(h0, 0, HX, 0, 1))
+        pl.when(gy == ngy - 1)(lambda: clear(h0, 0, HX, NYL + 1, NYL + 2))
 
     def layer_b(sec, g, gx0, gy0):
-        def body(yt, carry):
-            y0 = 4 * yt
-            pairs = [(0, y0), (2, y0)]
-            v = leaky(boxes(2 * sec + 1, (hm, h0, hp), pairs)).astype(BF)
-            for k, (x0, _) in enumerate(pairs):
-                b = v[:, L * k:L * k + L].reshape(2, 4, C, L)
-                for xq in range(2):
-                    g[gx0 + x0 + xq, pl.ds(gy0 + y0, 4)] = b[xq]
-            return carry
-        lax.fori_loop(0, NYL // 4, body, 0)
+        layer(2 * sec + 1, (hm, h0, hp), lambda j: (2 * lax.rem(j, 2), 4 * lax.div(j, 2)), 16, g, gx0, gy0)
 
     def to_stage(q, g, gx0, gy0):
         for y in range(NYL // 16):
@@ -366,13 +375,17 @@
     wcopy(1, ball, 1 - seg).wait_recv()
     wcopy(0, wall).wait_send()
     wcopy(1, ball).wait_send()
+    lax.fori_loop(0, HY + 1, table_s, 0)
+    for f in (fm, fp):
+        clear(f, 0, FX, NYL + 4, FY)
     for sec in range(2):
         make_weights(sec)
     end_exchange(0, f1, eb1, yb1)
 
-    shift_rows(f1, eb1)
+    shift(f1, eb1[1], FX, 0, fm, fp)
     strips(0, eb1)
     layer_a(0, f1)
+    shift(h0, hn[...], HX, 1, hm, hp)
     layer_b(0, f2, 2, 2)
 
     start_exchange(1, f2, eb2, yb2)
@@ -381,9 +394,10 @@
     middle_exchange(1, f2, eb2, yb2)
     end_exchange(1, f2, eb2, yb2)
 
-    shift_rows(f2, eb2)
+    shift(f2, eb2[1], FX, 0, fm, fp)
     strips(1, eb2)
     layer_a(1, f2)
+    shift(h0, hn[...], HX, 1, hm, hp)
     layer_b(1, res, 0, 0)
     to_stage(1, res, 0, 0)
     send_out(1)
@@ -428,6 +442,9 @@
             pltpu.VMEM((48, 256), F32),
             pltpu.VMEM((256, 256), BF),
             pltpu.VMEM((L, L), BF),
+            pltpu.VMEM((L, 2 * L), BF),
+            pltpu.VMEM((HY + 1, L, 2 * L), BF),
+            pltpu.VMEM((NYL * L, L), BF),
             pltpu.VMEM((2, FX, C, L), BF),
             pltpu.VMEM((2, FX, C, L), BF),
             pltpu.VMEM((2, 2, NXL, C, L), BF),

time: 56.9 us -> 50.7 us (0.89)
  the two profiles are of different devices: /device:TPU:7 before, /device:TPU:69 now
where the time goes in v2:
time: 50.7 us; the launch traced here: 50.6 us
  Pallas kernels  48.2 us (95%)
  local copies, waits for them, and re-layouts  2.31 us (5%)
    pallas_call x1, Pallas kernels, shards(): pl.pallas_call(functools.partial(kernel, sizes), name='sections', out_sha...  48.2 us
    unnamed x1, local copies, waits for them, and re-layouts  2.31 us

profile of v2, /device:TPU:69, one launch (start us, length us, event | category | flops | bytes accessed | tf_op | source)
XLA Modules:
  0.0 50.6 jit_solution(8997886643100144683)
XLA Ops:
  0.0 48.2 %sections.1 = bf16[2,16,4,32,128]{4,3,2,1,0:T(8,128)(2,1)} custom-call(bf16[2,16,4,32,128]{4,3,2,1,0:T(8,128)(2,1)} %feat.1, bf16[2,27,16,16]{3,2,1,0:T(8,128)(2,1)} %bitcast.8, bf16[2,16]{1,0:T(2,128)(2,1)} %bitcast.9), custom_call_target="tpu_custom_call" | custom-call | tf_op jit(solution)/shard_map/sections/pallas_call | solution.py:421
  48.3 2.3 %copy.5 = bf16[1,2,16,4,32,128]{5,4,3,2,1,0:T(8,128)(2,1)} copy(bf16[1,2,16,4,32,128]{5,4,3,2,1,0:T(8,128)(2,1)} %bitcast.7) | data formatting | bytes 2097152

commit v3 on v2

--- a/solution.py
+++ b/solution.py
@@ -35,7 +35,7 @@
 
 def kernel(
     sizes, feat, wts, bias, out,
-    raw, wall, ball, f1, f2, fm, fp, h0, hm, hp, tm, ws, base, brow, wbase, pm, ones, sh, sy, xe,
+    raw, wall, ball, f1, f2, fm, fp, h0, hm, hp, tm, ws, base, brow, wbase, pm, ones, xe,
     eb1, eb2, yb1, yb2, hn, res, stage,
     lsem, wsem, wrs, ssx, rsx, ssy, rsy, ssz, rsz, sso, rso,
 ):
@@ -100,12 +100,6 @@
     pm[...] = jnp.where((r // 16 == c % 16) & (r % 16 == c // 16), 1.0, 0.0).astype(BF)
     orow = lax.broadcasted_iota(jnp.int32, (L, L), 0)
     ones[...] = jnp.where(orow < C, 1.0, 0.0).astype(BF)
-    rl, cl = iota((L, 2 * L), 0), iota((L, 2 * L), 1)
-    sh[...] = one_hot((cl < L) & (rl == cl - 1) | (cl >= L) & (rl == cl - L + 1))
-    target = jnp.where(gz == 0, 2 * L - 1, 0)
-    def table_s(i, carry):
-        sy[i] = one_hot((rl == i) & (cl == target))
-        return carry
     re, ce = iota((L, L), 0), iota((L, L), 1)
     def table_e(y, carry):
         hit = (re == edge) & (ce == y + 2) | (re == inner) & (ce == y + 66)
@@ -161,9 +155,6 @@
         return pltpu.make_async_remote_copy(
             stage.at[q], out.at[seg], sso.at[q], rso.at[q],
             device_id={"segment": 1 - seg}, device_id_type=MESH)
-
-    def lcopy(q):
-        return pltpu.make_async_copy(stage.at[q], out.at[seg], lsem.at[3 + q])
 
     def wcopy(k, ref, sec=seg):
         return pltpu.make_async_remote_copy(
@@ -275,18 +266,16 @@
                 wbase[16:32, 144:160] = diag[0:16, 0:16].astype(F32)
                 ws[sec] = wbase[...].astype(BF)
 
-    def shift(src, edges, n, first, dm, dp):
-        def body(i, carry):
-            e = edges.reshape(n * C, L)
-            for k in range(4):
-                y = 4 * i + k
-                lhs = jnp.concatenate([src[:, y].reshape(n * C, L), e], axis=1)
-                rhs = jnp.concatenate([sh[...], sy[first + y]], axis=0)
-                t = dots(lhs, rhs).astype(BF)
-                dm[:, y] = t[:, :L].reshape(n, C, L)
-                dp[:, y] = t[:, L:].reshape(n, C, L)
-            return carry
-        lax.fori_loop(0, HY // 4, body, 0)
+    def shifted(v, n, lane):
+        h = jnp.where(lanes == edge, pltpu.roll(n, (L - lane) % L, 1) if lane else n, zrow)
+        return (jnp.where(lanes == 0, h, pltpu.roll(v, 1, 1)),
+                jnp.where(lanes == L - 1, h, pltpu.roll(v, L - 1, 1)))
+
+    def shift(f, eb, planes):
+        for x in planes:
+            n = pltpu.roll(eb[1, x], edge, 1)
+            for y in range(NYL + 4):
+                fm[x, y], fp[x, y] = shifted(f[x, y], n, y)
 
     def strips(sec, eb):
         one = ones[0:C, :]
@@ -322,47 +311,52 @@
             acc = t if acc is None else acc + t
         return leaky(acc).astype(BF)
 
-    def layer(lay, fields, todo, n, dst, ox, oy):
-        def body(i, carry):
-            pairs = [todo(4 * i + k) for k in range(4)]
-            for h in range(2):
-                v = boxes(lay, fields, pairs[2 * h:2 * h + 2])
-                for k in range(2):
-                    x0, y0 = pairs[2 * h + k]
-                    b = v[:, L * k:L * k + L].reshape(2, 4, C, L)
-                    for xq in range(2):
-                        dst[ox + x0 + xq, pl.ds(oy + y0, 4)] = b[xq]
-            return carry
-        lax.fori_loop(0, (n + 3) // 4, body, 0)
-
-    def layer_a(sec, f):
-        def todo(j):
-            j = jnp.minimum(j, 26)
-            return 2 * lax.rem(j, 3), 4 * lax.div(j, 3)
-        layer(2 * sec, (fm, f, fp), todo, 27, h0, 0, 0)
-        pl.when(gx == 0)(lambda: clear(h0, 0, 1, 0, HY))
-        pl.when(gx == ngx - 1)(lambda: clear(h0, HX - 1, HX, 0, HY))
-        pl.when(gy == 0)(lambda: clear(h0, 0, HX, 0, 1))
-        pl.when(gy == ngy - 1)(lambda: clear(h0, 0, HX, NYL + 1, NYL + 2))
-
-    def layer_b(sec, g, gx0, gy0):
-        layer(2 * sec + 1, (hm, h0, hp), lambda j: (2 * lax.rem(j, 2), 4 * lax.div(j, 2)), 16, g, gx0, gy0)
-
-    def to_stage(q, g, gx0, gy0):
+    def layer_a(sec, f, todo):
+        ns = [pltpu.roll(hn[j], edge, 1) for j in range(HX)]
+        for h in range(0, len(todo), 2):
+            pairs = todo[h:h + 2]
+            v = boxes(2 * sec, (fm, f, fp), pairs)
+            for k, (x0, y0) in enumerate(pairs):
+                b = v[:, L * k:L * k + L].reshape(2, 4, C, L)
+                for xq in range(2):
+                    for yq in range(4):
+                        x, y = x0 + xq, y0 + yq
+                        h0[x, y] = b[xq, yq]
+                        hm[x, y], hp[x, y] = shifted(b[xq, yq], ns[x], y + 1)
+        for r in (h0, hm, hp):
+            pl.when(gx == 0)(lambda r=r: clear(r, 0, 1, 0, HY))
+            pl.when(gx == ngx - 1)(lambda r=r: clear(r, HX - 1, HX, 0, HY))
+            pl.when(gy == 0)(lambda r=r: clear(r, 0, HX, 0, 1))
+            pl.when(gy == ngy - 1)(lambda r=r: clear(r, 0, HX, NYL + 1, NYL + 2))
+
+    def layer_b(sec, g, gx0, gy0, todo):
+        for h in range(0, len(todo), 2):
+            pairs = todo[h:h + 2]
+            v = boxes(2 * sec + 1, (hm, h0, hp), pairs)
+            for k, (x0, y0) in enumerate(pairs):
+                b = v[:, L * k:L * k + L].reshape(2, 4, C, L)
+                for xq in range(2):
+                    g[gx0 + x0 + xq, pl.ds(gy0 + y0, 4)] = b[xq]
+
+    def channels_first(g, gx0, gy0, dst):
         for y in range(NYL // 16):
             for x in range(0, NXL, 2):
                 ab = [g[gx0 + x + k, pl.ds(gy0 + 16 * y, 16)].reshape(256, L) for k in range(2)]
                 t = dots(pm[...], jnp.concatenate(ab, axis=1)).astype(BF)
                 for k in range(2):
-                    stage[q, :, x + k, 16 * y:16 * y + 16, :] = t[:, L * k:L * k + L].reshape(C, 16, L)
-
-    def send_out(q):
+                    dst[:, x + k, 16 * y:16 * y + 16, :] = t[:, L * k:L * k + L].reshape(C, 16, L)
+
+    def send_out(q, g, gx0, gy0):
         @pl.when(seg == q)
         def _():
-            lcopy(q).start()
+            channels_first(g, gx0, gy0, out.at[seg])
         @pl.when(seg != q)
         def _():
+            channels_first(g, gx0, gy0, stage.at[q])
             ocopy(q).start()
+
+    def boxes_of(xs, ny):
+        return [(x, y) for y in range(0, ny, 4) for x in xs]
 
     start_exchange(0, f1, eb1, yb1)
     wl.wait()
@@ -375,37 +369,31 @@
     wcopy(1, ball, 1 - seg).wait_recv()
     wcopy(0, wall).wait_send()
     wcopy(1, ball).wait_send()
-    lax.fori_loop(0, HY + 1, table_s, 0)
     for f in (fm, fp):
         clear(f, 0, FX, NYL + 4, FY)
     for sec in range(2):
         make_weights(sec)
     end_exchange(0, f1, eb1, yb1)
 
-    shift(f1, eb1[1], FX, 0, fm, fp)
+    shift(f1, eb1, range(FX))
     strips(0, eb1)
-    layer_a(0, f1)
-    shift(h0, hn[...], HX, 1, hm, hp)
-    layer_b(0, f2, 2, 2)
+    layer_a(0, f1, boxes_of((0, 2, 4), HY))
+    layer_b(0, f2, 2, 2, boxes_of((0, 2), NYL))
 
     start_exchange(1, f2, eb2, yb2)
-    to_stage(0, f2, 2, 2)
-    send_out(0)
+    send_out(0, f2, 2, 2)
     middle_exchange(1, f2, eb2, yb2)
     end_exchange(1, f2, eb2, yb2)
 
-    shift(f2, eb2[1], FX, 0, fm, fp)
+    shift(f2, eb2, range(FX))
     strips(1, eb2)
-    layer_a(1, f2)
-    shift(h0, hn[...], HX, 1, hm, hp)
-    layer_b(1, res, 0, 0)
-    to_stage(1, res, 0, 0)
-    send_out(1)
+    layer_a(1, f2, boxes_of((0, 2, 4), HY))
+    layer_b(1, res, 0, 0, boxes_of((0, 2), NYL))
+    send_out(1, res, 0, 0)
 
     for q in range(2):
         @pl.when(seg == q)
         def _(q=q):
-            lcopy(q).wait()
             pltpu.make_async_remote_copy(
                 stage.at[q], out.at[1 - seg], sso.at[q], rso.at[q],
                 device_id={"segment": 1 - seg}, device_id_type=MESH).wait_recv()
@@ -416,14 +404,14 @@
 
 def shards(sizes, features, weights, biases):
     w = weights[0].transpose(0, 3, 4, 5, 1, 2).reshape(2, 27, C, C)
-    any_space = pl.BlockSpec(memory_space=pl.ANY)
+    hbm = pl.BlockSpec(memory_space=pltpu.HBM)
     dma = pltpu.SemaphoreType.DMA
     out = pl.pallas_call(
         functools.partial(kernel, sizes),
         name="sections",
         out_shape=jax.ShapeDtypeStruct((2, C, NXL, NYL, L), BF),
-        in_specs=[any_space] * 3,
-        out_specs=any_space,
+        in_specs=[hbm] * 3,
+        out_specs=pl.BlockSpec(memory_space=pltpu.VMEM),
         scratch_shapes=[
             pltpu.VMEM((C, NXL, NYL, L), BF),
             pltpu.VMEM((2, 2, 27, C, C), BF),
@@ -442,8 +430,6 @@
             pltpu.VMEM((48, 256), F32),
             pltpu.VMEM((256, 256), BF),
             pltpu.VMEM((L, L), BF),
-            pltpu.VMEM((L, 2 * L), BF),
-            pltpu.VMEM((HY + 1, L, 2 * L), BF),
             pltpu.VMEM((NYL * L, L), BF),
             pltpu.VMEM((2, FX, C, L), BF),
             pltpu.VMEM((2, FX, C, L), BF),
@@ -452,14 +438,14 @@
             pltpu.VMEM((HX, C, L), BF),
             pltpu.VMEM((NXL, NYL, C, L), BF),
             pltpu.VMEM((2, C, NXL, NYL, L), BF),
-            dma((5,)), dma((2,)), dma((2,)),
+            dma((3,)), dma((2,)), dma((2,)),
             dma((2, 2, 5)), dma((2, 2, 5)),
             dma((2, 2, 2)), dma((2, 2, 2)),
             dma((2,)), dma((2,)), dma((2,)), dma((2,)),
         ],
         compiler_params=pltpu.CompilerParams(
-            collective_id=0, has_side_effects=True, vmem_limit_bytes=60 << 20),
-    )(features, w, biases[0])
+            collective_id=0, has_side_effects=True, vmem_limit_bytes=32 << 20),
+    )(*(pltpu.with_memory_space_constraint(a, pltpu.HBM) for a in (features, w, biases[0])))
     return out[None]
 
 

time: 50.7 us -> 38.1 us (0.75)
  Pallas kernels: 48.2 us -> 37.1 us
  local copies, waits for them, and re-layouts: 2.31 us -> 0.97 us
    pallas_call x1, Pallas kernels: 48.2 us -> 37.1 us  [shards(): pl.pallas_call(functools.partial(kernel, sizes), name='sections', out_sha...]
    unnamed x1, local copies, waits for them, and re-layouts: 2.31 us -> 0.97 us
where the time goes in v3:
time: 38.1 us; the launch traced here: 38 us
  Pallas kernels  37.1 us (97%)
  local copies, waits for them, and re-layouts  0.97 us (3%)
    pallas_call x1, Pallas kernels, shards(): pl.pallas_call(functools.partial(kernel, sizes), name='sections', out_sha...  37.1 us
    unnamed x1, local copies, waits for them, and re-layouts  0.97 us

profile of v3, /device:TPU:69, one launch (start us, length us, event | category | flops | bytes accessed | tf_op | source)
XLA Modules:
  0.0 38.0 jit_solution(12133941187646689830)
XLA Ops:
  0.0 37.1 %sections.1 = bf16[2,16,4,32,128]{4,3,2,1,0:T(8,128)(2,1)S(1)} custom-call(bf16[2,16,4,32,128]{4,3,2,1,0:T(8,128)(2,1)} %feat.1, bf16[2,27,16,16]{3,2,1,0:T(8,128)(2,1)} %bitcast.8, bf16[2,16]{1,0:T(2,128)(2,1)} %bitcast.9), custom_call_target="tpu_custom_call" | custom-call | tf_op jit(solution)/shard_map/sections/pallas_call | solution.py:409
  37.1 1.0 %copy.5 = bf16[1,2,16,4,32,128]{5,4,3,2,1,0:T(8,128)(2,1)} copy(bf16[1,2,16,4,32,128]{5,4,3,2,1,0:T(8,128)(2,1)S(1)} %bitcast.7) | data formatting | bytes 2097152

commit v4 on v3

--- a/solution.py
+++ b/solution.py
@@ -37,7 +37,7 @@
     sizes, feat, wts, bias, out,
     raw, wall, ball, f1, f2, fm, fp, h0, hm, hp, tm, ws, base, brow, wbase, pm, ones, xe,
     eb1, eb2, yb1, yb2, hn, res, stage,
-    lsem, wsem, wrs, ssx, rsx, ssy, rsy, ssz, rsz, sso, rso,
+    lsem, wsem, wrs, ssx, rsx, ssy, rsy, sse, rse, ssz, rsz, sso, rso,
 ):
     ngx, ngy = sizes
     seg, gx = lax.axis_index("segment"), lax.axis_index("gx")
@@ -92,6 +92,9 @@
         @pl.when(ok)
         def _(axis=axis, step=step):
             pl.semaphore_signal(bar, inc=1, device_id=to(axis, step), device_id_type=MESH)
+            if axis == "y":
+                pl.semaphore_signal(
+                    bar, inc=1, device_id={"gy": gy + step, "gz": 1 - gz}, device_id_type=MESH)
     pl.semaphore_signal(bar, inc=1, device_id={"gz": 1 - gz}, device_id_type=MESH)
     pl.semaphore_signal(bar, inc=1, device_id={"segment": 1 - seg}, device_id_type=MESH)
 
@@ -114,41 +117,41 @@
             for k in range(2):
                 f1[x + k + 2, pl.ds(2 + 16 * y, 16)] = t[:, L * k:L * k + L].reshape(16, C, L)
 
-    count = 2 + sum(jnp.where(ok, 1, 0) for ok in has.values())
+    count = 2 + sum(
+        jnp.where(ok, 2 if axis == "y" else 1, 0) for (axis, _), ok in has.items())
     pl.semaphore_wait(bar, count)
 
-    def xcopy(q, f, eb, step, k):
+    def xcopy(q, f, eb, step, half, k):
         d = 0 if step > 0 else 1
         mv = -NXL * step
-        near, far = (FX - 3, FX - 4) if step > 0 else (2, 3)
-        lo = FX - 4 if step > 0 else 2
+        src = (FX - 3, FX - 4)[half] if step > 0 else (2, 3)[half]
         part = (
-            lambda o: f.at[near + o, pl.ds(2, NYL)],
-            lambda o: f.at[far + o, pl.ds(2, NYL)],
-            lambda o: f.at[pl.ds(lo + o, 2), pl.ds(0, 2)],
-            lambda o: f.at[pl.ds(lo + o, 2), pl.ds(NYL + 2, 2)],
-            lambda o: eb.at[:, pl.ds(lo + o, 2)],
+            lambda x: f.at[x, pl.ds(2, NYL)],
+            lambda x: f.at[x, pl.ds(0, 2)],
+            lambda x: f.at[x, pl.ds(NYL + 2, 2)],
+            lambda x: eb.at[:, x],
         )[k]
         return pltpu.make_async_remote_copy(
-            part(0), part(mv), ssx.at[q, d, k], rsx.at[q, d, k],
+            part(src), part(src + mv), ssx.at[q, d, half, k], rsx.at[q, d, half, k],
             device_id=to("x", step), device_id_type=MESH)
 
-    def yrows(q, f, step):
+    def yrows(q, f, step, p):
         d = 0 if step > 0 else 1
         src, dst = (NYL, 0) if step > 0 else (2, NYL + 2)
         return pltpu.make_async_remote_copy(
-            f.at[pl.ds(2, NXL), pl.ds(src, 2)], f.at[pl.ds(2, NXL), pl.ds(dst, 2)],
-            ssy.at[q, d, 0], rsy.at[q, d, 0], device_id=to("y", step), device_id_type=MESH)
-
-    def yedges(q, eb, yb, step):
+            f.at[2 + p, pl.ds(src, 2)], f.at[2 + p, pl.ds(dst, 2)],
+            ssy.at[q, d, p], rsy.at[q, d, p], device_id=to("y", step), device_id_type=MESH)
+
+    def yedges(q, eb, yb, step, other, p):
         d = 0 if step > 0 else 1
         return pltpu.make_async_remote_copy(
-            eb.at[:, pl.ds(2, NXL)], yb.at[d],
-            ssy.at[q, d, 1], rsy.at[q, d, 1], device_id=to("y", step), device_id_type=MESH)
-
-    def zcopy(q, eb):
+            eb.at[0, 2 + p], yb.at[d, other, p],
+            sse.at[q, d, other, p], rse.at[q, d, other, p],
+            device_id={"gy": gy + step, "gz": 1 - gz if other else gz}, device_id_type=MESH)
+
+    def zcopy(q, eb, p):
         return pltpu.make_async_remote_copy(
-            eb.at[0, pl.ds(2, NXL)], eb.at[1, pl.ds(2, NXL)], ssz.at[q], rsz.at[q],
+            eb.at[0, 2 + p], eb.at[1, 2 + p], ssz.at[q, p], rsz.at[q, p],
             device_id={"gz": 1 - gz}, device_id_type=MESH)
 
     def ocopy(q):
@@ -162,75 +165,84 @@
             device_id={"segment": 1 - seg}, device_id_type=MESH)
 
 
-    def pack_edges(f, eb):
+    def pack_edges(f, eb, planes):
         acc = None
         for y in range(0, NYL, 2):
-            lhs = [f[pl.ds(2, NXL), 2 + y + k].reshape(NXL * C, L) for k in range(2)]
+            lhs = [jnp.concatenate([f[2 + p, 2 + y + k] for p in planes], axis=0) for k in range(2)]
             t = dots(jnp.concatenate(lhs, axis=1), xe[pl.ds(L * y, 2 * L), :])
             acc = t if acc is None else acc + t
-        eb[0, pl.ds(2, NXL)] = acc.astype(BF).reshape(NXL, C, L)
-
-    def start_exchange(q, f, eb, yb):
+        acc = acc.astype(BF)
+        for i, p in enumerate(planes):
+            eb[0, 2 + p] = acc[C * i:C * i + C]
+
+    def each(axis, turn, work):
         for step in (1, -1):
-            @pl.when(has["x", step])
-            def _(step=step):
-                xcopy(q, f, eb, step, 0).start()
-                xcopy(q, f, eb, step, 1).start()
-        for step in (1, -1):
-            @pl.when(has["y", step])
-            def _(step=step):
-                yrows(q, f, step).start()
-        pack_edges(f, eb)
-        zcopy(q, eb).start()
-
-    def middle_exchange(q, f, eb, yb):
-        for step in (1, -1):
-            @pl.when(has["y", -step])
-            def _(step=step):
-                yrows(q, f, step).wait_recv()
-        for step in (1, -1):
-            @pl.when(has["x", step])
-            def _(step=step):
-                xcopy(q, f, eb, step, 2).start()
-                xcopy(q, f, eb, step, 3).start()
-        zcopy(q, eb).wait_recv()
-        zcopy(q, eb).wait_send()
-        for step in (1, -1):
-            @pl.when(has["y", step])
-            def _(step=step):
-                yedges(q, eb, yb, step).start()
-        for step in (1, -1):
-            @pl.when(has["y", -step])
-            def _(step=step):
-                yedges(q, eb, yb, step).wait_recv()
-            @pl.when(has["y", step])
-            def _(step=step):
-                yedges(q, eb, yb, step).wait_send()
+            pl.when(has[axis, turn * step])(lambda step=step: work(step))
+
+    def start_faces(q, f, eb, half):
+        each("x", 1, lambda step: xcopy(q, f, eb, step, half, 0).start())
+
+    def start_sides(q, f, eb, yb, planes):
+        def rows(step):
+            for p in planes:
+                yrows(q, f, step, p).start()
+        each("y", 1, rows)
+        pack_edges(f, eb, planes)
+        for p in planes:
+            zcopy(q, eb, p).start()
+        def strips_out(step):
+            for p in planes:
+                for other in range(2):
+                    yedges(q, eb, yb, step, other, p).start()
+        each("y", 1, strips_out)
+
+    def pass_on(q, f, eb, yb, planes, half):
+        def rows_in(step):
+            for p in planes:
+                yrows(q, f, step, p).wait_recv()
+        each("y", -1, rows_in)
+        def rows_on(step):
+            xcopy(q, f, eb, step, half, 1).start()
+            xcopy(q, f, eb, step, half, 2).start()
+        each("x", 1, rows_on)
+        for p in planes:
+            zcopy(q, eb, p).wait_recv()
+            zcopy(q, eb, p).wait_send()
+        def strips_in(step):
+            for p in planes:
+                for other in range(2):
+                    yedges(q, eb, yb, step, other, p).wait_recv()
+        each("y", -1, strips_in)
+        def strips_gone(step):
+            for p in planes:
+                for other in range(2):
+                    yedges(q, eb, yb, step, other, p).wait_send()
+        each("y", 1, strips_gone)
         low = lanes % 64
         for s in range(2):
-            for x in range(NXL):
-                v = eb[s, x + 2]
-                v = jnp.where(low < 2, pltpu.roll(yb[0, s, x], L - NYL, 1), v)
-                v = jnp.where((low >= NYL + 2) & (low < NYL + 4), pltpu.roll(yb[1, s, x], NYL, 1), v)
-                eb[s, x + 2] = v
-        for step in (1, -1):
-            @pl.when(has["x", step])
-            def _(step=step):
-                xcopy(q, f, eb, step, 4).start()
-
-    def end_exchange(q, f, eb, yb):
-        for step in (1, -1):
-            @pl.when(has["x", -step])
-            def _(step=step):
-                for k in range(5):
-                    xcopy(q, f, eb, step, k).wait_recv()
-            @pl.when(has["x", step])
-            def _(step=step):
-                for k in range(5):
-                    xcopy(q, f, eb, step, k).wait_send()
-            @pl.when(has["y", step])
-            def _(step=step):
-                yrows(q, f, step).wait_send()
+            for p in planes:
+                v = eb[s, p + 2]
+                v = jnp.where(low < 2, pltpu.roll(yb[0, s, p], L - NYL, 1), v)
+                v = jnp.where((low >= NYL + 2) & (low < NYL + 4), pltpu.roll(yb[1, s, p], NYL, 1), v)
+                eb[s, p + 2] = v
+        each("x", 1, lambda step: xcopy(q, f, eb, step, half, 3).start())
+
+    def arrive(q, f, eb, half):
+        def come(step):
+            for k in range(4):
+                xcopy(q, f, eb, step, half, k).wait_recv()
+        each("x", -1, come)
+
+    def drain(q, f, eb):
+        def xgone(step):
+            for half in range(2):
+                for k in range(4):
+                    xcopy(q, f, eb, step, half, k).wait_send()
+        each("x", 1, xgone)
+        def ygone(step):
+            for p in range(NXL):
+                yrows(q, f, step, p).wait_send()
+        each("y", 1, ygone)
 
     def make_weights(sec):
         for lay in range(2):
@@ -277,11 +289,11 @@
             for y in range(NYL + 4):
                 fm[x, y], fp[x, y] = shifted(f[x, y], n, y)
 
-    def strips(sec, eb):
+    def strips(sec, eb, todo):
         one = ones[0:C, :]
         tail = jnp.zeros((256 - 160, L), BF)
         lane = lax.broadcasted_iota(jnp.int32, (C, L), 1)
-        for j in range(HX):
+        for j in todo:
             rows = []
             for dx in range(3):
                 rows += [eb[0, j + dx], eb[1, j + dx], pltpu.roll(eb[1, j + dx], 64, 1)]
@@ -295,7 +307,7 @@
                 bad = bad | (gx == ngx - 1)
             hn[j] = jnp.where(bad, 0.0, v).astype(BF)
 
-    def boxes(lay, fields, pairs):
+    def boxes(lay, fields, pairs, xqs):
         acc = None
         for k in range(5):
             cols = []
@@ -307,36 +319,39 @@
                 if k == 4:
                     rows.append(ones[...])
                 cols.append(jnp.concatenate(rows, axis=0))
-            t = dots(tm[lay, :, 256 * k:256 * k + 256], jnp.concatenate(cols, axis=1))
+            t = dots(tm[lay, 64 * xqs[0]:64 * xqs[-1] + 64, 256 * k:256 * k + 256], jnp.concatenate(cols, axis=1))
             acc = t if acc is None else acc + t
         return leaky(acc).astype(BF)
 
-    def layer_a(sec, f, todo):
-        ns = [pltpu.roll(hn[j], edge, 1) for j in range(HX)]
+    def layer(lay, fields, todo, xqs, put):
         for h in range(0, len(todo), 2):
             pairs = todo[h:h + 2]
-            v = boxes(2 * sec, (fm, f, fp), pairs)
+            v = boxes(lay, fields, pairs, xqs)
             for k, (x0, y0) in enumerate(pairs):
-                b = v[:, L * k:L * k + L].reshape(2, 4, C, L)
-                for xq in range(2):
+                b = v[:, L * k:L * k + L].reshape(len(xqs), 4, C, L)
+                for i, xq in enumerate(xqs):
                     for yq in range(4):
-                        x, y = x0 + xq, y0 + yq
-                        h0[x, y] = b[xq, yq]
-                        hm[x, y], hp[x, y] = shifted(b[xq, yq], ns[x], y + 1)
+                        put(x0 + xq, y0 + yq, b[i, yq])
+
+    def layer_a(sec, f, todo, xqs=(0, 1)):
+        xs = sorted({x0 + xq for x0, _ in todo for xq in xqs})
+        ns = {x: pltpu.roll(hn[x], edge, 1) for x in xs}
+        def put(x, y, t):
+            h0[x, y] = t
+            hm[x, y], hp[x, y] = shifted(t, ns[x], y + 1)
+        layer(2 * sec, (fm, f, fp), todo, xqs, put)
+
+    def outside():
         for r in (h0, hm, hp):
             pl.when(gx == 0)(lambda r=r: clear(r, 0, 1, 0, HY))
             pl.when(gx == ngx - 1)(lambda r=r: clear(r, HX - 1, HX, 0, HY))
             pl.when(gy == 0)(lambda r=r: clear(r, 0, HX, 0, 1))
             pl.when(gy == ngy - 1)(lambda r=r: clear(r, 0, HX, NYL + 1, NYL + 2))
 
-    def layer_b(sec, g, gx0, gy0, todo):
-        for h in range(0, len(todo), 2):
-            pairs = todo[h:h + 2]
-            v = boxes(2 * sec + 1, (hm, h0, hp), pairs)
-            for k, (x0, y0) in enumerate(pairs):
-                b = v[:, L * k:L * k + L].reshape(2, 4, C, L)
-                for xq in range(2):
-                    g[gx0 + x0 + xq, pl.ds(gy0 + y0, 4)] = b[xq]
+    def layer_b(sec, g, o, todo, xqs=(0, 1)):
+        def put(x, y, t):
+            g[o + x, o + y] = t
+        layer(2 * sec + 1, (hm, h0, hp), todo, xqs, put)
 
     def channels_first(g, gx0, gy0, dst):
         for y in range(NYL // 16):
@@ -358,12 +373,16 @@
     def boxes_of(xs, ny):
         return [(x, y) for y in range(0, ny, 4) for x in xs]
 
-    start_exchange(0, f1, eb1, yb1)
+    near, far = (0, 3), (1, 2)
+    start_faces(0, f1, eb1, 0)
+    start_sides(0, f1, eb1, yb1, (0, 1, 2, 3))
     wl.wait()
     bl.wait()
     wcopy(0, wall).start()
     wcopy(1, ball).start()
-    middle_exchange(0, f1, eb1, yb1)
+    pass_on(0, f1, eb1, yb1, near, 0)
+    start_faces(0, f1, eb1, 1)
+    pass_on(0, f1, eb1, yb1, far, 1)
     brow[...] = jnp.zeros_like(brow)
     wcopy(0, wall, 1 - seg).wait_recv()
     wcopy(1, ball, 1 - seg).wait_recv()
@@ -373,23 +392,43 @@
         clear(f, 0, FX, NYL + 4, FY)
     for sec in range(2):
         make_weights(sec)
-    end_exchange(0, f1, eb1, yb1)
-
-    shift(f1, eb1, range(FX))
-    strips(0, eb1)
-    layer_a(0, f1, boxes_of((0, 2, 4), HY))
-    layer_b(0, f2, 2, 2, boxes_of((0, 2), NYL))
-
-    start_exchange(1, f2, eb2, yb2)
+
+    arrive(0, f1, eb1, 0)
+    shift(f1, eb1, range(1, FX - 1))
+    strips(0, eb1, range(1, HX - 1))
+    layer_a(0, f1, boxes_of((1, 3), HY))
+    outside()
+    layer_b(0, f2, 2, boxes_of((1,), NYL))
+    start_faces(1, f2, eb2, 1)
+    start_sides(1, f2, eb2, yb2, far)
+    arrive(0, f1, eb1, 1)
+    shift(f1, eb1, (0, FX - 1))
+    strips(0, eb1, (0, HX - 1))
+    layer_a(0, f1, boxes_of((0,), HY), (0,))
+    layer_a(0, f1, boxes_of((4,), HY), (1,))
+    outside()
+    layer_b(0, f2, 2, boxes_of((0,), NYL), (0,))
+    layer_b(0, f2, 2, boxes_of((2,), NYL), (1,))
+
+    start_faces(1, f2, eb2, 0)
+    start_sides(1, f2, eb2, yb2, near)
     send_out(0, f2, 2, 2)
-    middle_exchange(1, f2, eb2, yb2)
-    end_exchange(1, f2, eb2, yb2)
-
-    shift(f2, eb2, range(FX))
-    strips(1, eb2)
-    layer_a(1, f2, boxes_of((0, 2, 4), HY))
-    layer_b(1, res, 0, 0, boxes_of((0, 2), NYL))
+    pass_on(1, f2, eb2, yb2, far, 1)
+    pass_on(1, f2, eb2, yb2, near, 0)
+    shift(f2, eb2, range(2, FX - 2))
+    strips(1, eb2, (2, 3))
+    layer_a(1, f2, boxes_of((2,), HY))
+    arrive(1, f2, eb2, 1)
+    shift(f2, eb2, (0, FX - 1))
+    arrive(1, f2, eb2, 0)
+    shift(f2, eb2, (1, FX - 2))
+    strips(1, eb2, (0, 1, 4, 5))
+    layer_a(1, f2, boxes_of((0, 4), HY))
+    outside()
+    layer_b(1, res, 0, boxes_of((0, 2), NYL))
     send_out(1, res, 0, 0)
+    drain(0, f1, eb1)
+    drain(1, f2, eb2)
 
     for q in range(2):
         @pl.when(seg == q)
@@ -439,9 +478,10 @@
             pltpu.VMEM((NXL, NYL, C, L), BF),
             pltpu.VMEM((2, C, NXL, NYL, L), BF),
             dma((3,)), dma((2,)), dma((2,)),
-            dma((2, 2, 5)), dma((2, 2, 5)),
-            dma((2, 2, 2)), dma((2, 2, 2)),
-            dma((2,)), dma((2,)), dma((2,)), dma((2,)),
+            dma((2, 2, 2, 4)), dma((2, 2, 2, 4)),
+            dma((2, 2, NXL)), dma((2, 2, NXL)),
+            dma((2, 2, 2, NXL)), dma((2, 2, 2, NXL)),
+            dma((2, NXL)), dma((2, NXL)), dma((2,)), dma((2,)),
         ],
         compiler_params=pltpu.CompilerParams(
             collective_id=0, has_side_effects=True, vmem_limit_bytes=32 << 20),

time: 38.1 us -> 34.6 us (0.908)
  the two profiles are of different devices: /device:TPU:69 before, /device:TPU:7 now
where the time goes in v4:
time: 34.6 us; the launch traced here: 34.5 us
  Pallas kernels  33.6 us (97%)
  local copies, waits for them, and re-layouts  0.97 us (3%)
    pallas_call x1, Pallas kernels, shards(): pl.pallas_call(functools.partial(kernel, sizes), name='sections', out_sha...  33.6 us
    unnamed x1, local copies, waits for them, and re-layouts  0.97 us

profile of v4, /device:TPU:7, one launch (start us, length us, event | category | flops | bytes accessed | tf_op | source)
XLA Modules:
  0.0 34.5 jit_solution(10929599870451415792)
XLA Ops:
  0.0 33.6 %sections.1 = bf16[2,16,4,32,128]{4,3,2,1,0:T(8,128)(2,1)S(1)} custom-call(bf16[2,16,4,32,128]{4,3,2,1,0:T(8,128)(2,1)} %feat.1, bf16[2,27,16,16]{3,2,1,0:T(8,128)(2,1)} %bitcast.8, bf16[2,16]{1,0:T(2,128)(2,1)} %bitcast.9), custom_call_target="tpu_custom_call" | custom-call | tf_op jit(solution)/shard_map/sections/pallas_call | solution.py:448
  33.6 1.0 %copy.5 = bf16[1,2,16,4,32,128]{5,4,3,2,1,0:T(8,128)(2,1)} copy(bf16[1,2,16,4,32,128]{5,4,3,2,1,0:T(8,128)(2,1)S(1)} %bitcast.7) | data formatting | bytes 2097152

commit v5 on v4

--- a/solution.py
+++ b/solution.py
@@ -14,6 +14,7 @@
 NXL, NYL, C, L = 4, 32, 16, 128
 FX, FY = NXL + 4, NYL + 6
 HX, HY = NXL + 2, NYL + 4
+CUT = (20, 16)
 KT = 1280
 
 
@@ -37,7 +38,7 @@
     sizes, feat, wts, bias, out,
     raw, wall, ball, f1, f2, fm, fp, h0, hm, hp, tm, ws, base, brow, wbase, pm, ones, xe,
     eb1, eb2, yb1, yb2, hn, res, stage,
-    lsem, wsem, wrs, ssx, rsx, ssy, rsy, sse, rse, ssz, rsz, sso, rso,
+    lsem, wsem, wrs, ssx, rsx, ssy, rsy, sse, rse, ssz, rsz, sso, rso, osem,
 ):
     ngx, ngy = sizes
     seg, gx = lax.axis_index("segment"), lax.axis_index("gx")
@@ -71,21 +72,32 @@
             return c
         lax.fori_loop(x0, x1, body, 0)
 
-    for f in (f1, f2):
-        clear(f, 0, FX, NYL + 4, FY)
-        pl.when(gx == 0)(lambda f=f: clear(f, 0, 2, 0, FY))
-        pl.when(gx == ngx - 1)(lambda f=f: clear(f, FX - 2, FX, 0, FY))
-        pl.when(gy == 0)(lambda f=f: clear(f, 0, FX, 0, 2))
-        pl.when(gy == ngy - 1)(lambda f=f: clear(f, 0, FX, NYL + 2, NYL + 4))
-    for e in (eb1, eb2):
-        for s in range(2):
-            for i in range(FX):
-                e[s, i] = zrow
-    for e in (yb1, yb2):
-        for d in range(2):
-            for s in range(2):
-                for i in range(NXL):
-                    e[d, s, i] = zrow
+    def clear_strips(eb, yb, planes, d):
+        for p in planes:
+            eb[0, p] = zrow
+            eb[1, p] = zrow
+        if d is not None:
+            for p in range(NXL):
+                yb[d, 0, p] = zrow
+                yb[d, 1, p] = zrow
+
+    for f, eb, yb in ((f1, eb1, yb1), (f2, eb2, yb2)):
+        @pl.when(gx == 0)
+        def _(f=f, eb=eb, yb=yb):
+            clear(f, 0, 2, 0, NYL + 4)
+            clear_strips(eb, yb, (0, 1), None)
+        @pl.when(gx == ngx - 1)
+        def _(f=f, eb=eb, yb=yb):
+            clear(f, FX - 2, FX, 0, NYL + 4)
+            clear_strips(eb, yb, (FX - 2, FX - 1), None)
+        @pl.when(gy == 0)
+        def _(f=f, eb=eb, yb=yb):
+            clear(f, 0, FX, 0, 2)
+            clear_strips(eb, yb, (), 0)
+        @pl.when(gy == ngy - 1)
+        def _(f=f, eb=eb, yb=yb):
+            clear(f, 0, FX, NYL + 2, NYL + 4)
+            clear_strips(eb, yb, (), 1)
 
     bar = pltpu.get_barrier_semaphore()
     for (axis, step), ok in has.items():
@@ -126,10 +138,11 @@
         mv = -NXL * step
         src = (FX - 3, FX - 4)[half] if step > 0 else (2, 3)[half]
         part = (
-            lambda x: f.at[x, pl.ds(2, NYL)],
+            lambda x: f.at[x, pl.ds(2, CUT[q])],
             lambda x: f.at[x, pl.ds(0, 2)],
             lambda x: f.at[x, pl.ds(NYL + 2, 2)],
             lambda x: eb.at[:, x],
+            lambda x: f.at[x, pl.ds(2 + CUT[q], NYL - CUT[q])],
         )[k]
         return pltpu.make_async_remote_copy(
             part(src), part(src + mv), ssx.at[q, d, half, k], rsx.at[q, d, half, k],
@@ -154,10 +167,18 @@
             eb.at[0, 2 + p], eb.at[1, 2 + p], ssz.at[q, p], rsz.at[q, p],
             device_id={"gz": 1 - gz}, device_id_type=MESH)
 
-    def ocopy(q):
+    def piece(ref, x, y):
+        return ref.at[:, pl.ds(x, 2), pl.ds(y, 16)]
+
+    def ocopy(q, x, y, slot=seg):
+        n = x // 2 + y // 8
         return pltpu.make_async_remote_copy(
-            stage.at[q], out.at[seg], sso.at[q], rso.at[q],
+            piece(stage.at[q], x, y), piece(out.at[slot], x, y), sso.at[q, n], rso.at[q, n],
             device_id={"segment": 1 - seg}, device_id_type=MESH)
+
+    def lcopy(q, x, y):
+        return pltpu.make_async_copy(
+            piece(stage.at[q], x, y), piece(out.at[seg], x, y), osem.at[q, x // 2 + y // 8])
 
     def wcopy(k, ref, sec=seg):
         return pltpu.make_async_remote_copy(
@@ -179,8 +200,11 @@
         for step in (1, -1):
             pl.when(has[axis, turn * step])(lambda step=step: work(step))
 
-    def start_faces(q, f, eb, half):
-        each("x", 1, lambda step: xcopy(q, f, eb, step, half, 0).start())
+    def start_faces(q, f, eb, half, parts=(0, 4)):
+        def go(step):
+            for k in parts:
+                xcopy(q, f, eb, step, half, k).start()
+        each("x", 1, go)
 
     def start_sides(q, f, eb, yb, planes):
         def rows(step):
@@ -227,16 +251,16 @@
                 eb[s, p + 2] = v
         each("x", 1, lambda step: xcopy(q, f, eb, step, half, 3).start())
 
-    def arrive(q, f, eb, half):
+    def arrive(q, f, eb, half, parts=range(5)):
         def come(step):
-            for k in range(4):
+            for k in parts:
                 xcopy(q, f, eb, step, half, k).wait_recv()
         each("x", -1, come)
 
     def drain(q, f, eb):
         def xgone(step):
             for half in range(2):
-                for k in range(4):
+                for k in range(5):
                     xcopy(q, f, eb, step, half, k).wait_send()
         each("x", 1, xgone)
         def ygone(step):
@@ -283,10 +307,10 @@
         return (jnp.where(lanes == 0, h, pltpu.roll(v, 1, 1)),
                 jnp.where(lanes == L - 1, h, pltpu.roll(v, L - 1, 1)))
 
-    def shift(f, eb, planes):
+    def shift(f, eb, planes, first=0, last=NYL + 4):
         for x in planes:
             n = pltpu.roll(eb[1, x], edge, 1)
-            for y in range(NYL + 4):
+            for y in range(first, last):
                 fm[x, y], fp[x, y] = shifted(f[x, y], n, y)
 
     def strips(sec, eb, todo):
@@ -353,25 +377,16 @@
             g[o + x, o + y] = t
         layer(2 * sec + 1, (hm, h0, hp), todo, xqs, put)
 
-    def channels_first(g, gx0, gy0, dst):
-        for y in range(NYL // 16):
-            for x in range(0, NXL, 2):
-                ab = [g[gx0 + x + k, pl.ds(gy0 + 16 * y, 16)].reshape(256, L) for k in range(2)]
-                t = dots(pm[...], jnp.concatenate(ab, axis=1)).astype(BF)
-                for k in range(2):
-                    dst[:, x + k, 16 * y:16 * y + 16, :] = t[:, L * k:L * k + L].reshape(C, 16, L)
-
-    def send_out(q, g, gx0, gy0):
-        @pl.when(seg == q)
-        def _():
-            channels_first(g, gx0, gy0, out.at[seg])
-        @pl.when(seg != q)
-        def _():
-            channels_first(g, gx0, gy0, stage.at[q])
-            ocopy(q).start()
-
-    def boxes_of(xs, ny):
-        return [(x, y) for y in range(0, ny, 4) for x in xs]
+    def send_out(q, g, o, x, y):
+        ab = [g[o + x + k, pl.ds(o + y, 16)].reshape(256, L) for k in range(2)]
+        t = dots(pm[...], jnp.concatenate(ab, axis=1)).astype(BF)
+        for k in range(2):
+            stage[q, :, x + k, y:y + 16, :] = t[:, L * k:L * k + L].reshape(C, 16, L)
+        pl.when(seg == q)(lambda: lcopy(q, x, y).start())
+        pl.when(seg != q)(lambda: ocopy(q, x, y).start())
+
+    def boxes_of(xs, ny, first=0):
+        return [(x, y) for y in range(first, ny, 4) for x in xs]
 
     near, far = (0, 3), (1, 2)
     start_faces(0, f1, eb1, 0)
@@ -381,14 +396,14 @@
     wcopy(0, wall).start()
     wcopy(1, ball).start()
     pass_on(0, f1, eb1, yb1, near, 0)
+    pass_on(0, f1, eb1, yb1, far, 1)
     start_faces(0, f1, eb1, 1)
-    pass_on(0, f1, eb1, yb1, far, 1)
     brow[...] = jnp.zeros_like(brow)
     wcopy(0, wall, 1 - seg).wait_recv()
     wcopy(1, ball, 1 - seg).wait_recv()
     wcopy(0, wall).wait_send()
     wcopy(1, ball).wait_send()
-    for f in (fm, fp):
+    for f in (f1, f2, fm, fp):
         clear(f, 0, FX, NYL + 4, FY)
     for sec in range(2):
         make_weights(sec)
@@ -401,18 +416,22 @@
     layer_b(0, f2, 2, boxes_of((1,), NYL))
     start_faces(1, f2, eb2, 1)
     start_sides(1, f2, eb2, yb2, far)
-    arrive(0, f1, eb1, 1)
-    shift(f1, eb1, (0, FX - 1))
-    strips(0, eb1, (0, HX - 1))
-    layer_a(0, f1, boxes_of((0,), HY), (0,))
-    layer_a(0, f1, boxes_of((4,), HY), (1,))
-    outside()
-    layer_b(0, f2, 2, boxes_of((0,), NYL), (0,))
-    layer_b(0, f2, 2, boxes_of((2,), NYL), (1,))
-
-    start_faces(1, f2, eb2, 0)
+    for part, (y0, y1, y2) in enumerate(((0, 20, 16), (20, HY, NYL))):
+        arrive(0, f1, eb1, 1, ((0, 1, 3), (2, 4))[part])
+        shift(f1, eb1, (0, FX - 1), (0, CUT[0] + 2)[part], (CUT[0] + 2, NYL + 4)[part])
+        if part == 0:
+            strips(0, eb1, (0, HX - 1))
+        layer_a(0, f1, boxes_of((0,), y1, y0), (0,))
+        layer_a(0, f1, boxes_of((4,), y1, y0), (1,))
+        outside()
+        layer_b(0, f2, 2, boxes_of((0,), y2, 16 * part), (0,))
+        layer_b(0, f2, 2, boxes_of((2,), y2, 16 * part), (1,))
+        start_faces(1, f2, eb2, 0, (4 * part,))
+
     start_sides(1, f2, eb2, yb2, near)
-    send_out(0, f2, 2, 2)
+    for y in (0, 16):
+        for x in (0, 2):
+            send_out(0, f2, 2, x, y)
     pass_on(1, f2, eb2, yb2, far, 1)
     pass_on(1, f2, eb2, yb2, near, 0)
     shift(f2, eb2, range(2, FX - 2))
@@ -425,20 +444,23 @@
     strips(1, eb2, (0, 1, 4, 5))
     layer_a(1, f2, boxes_of((0, 4), HY))
     outside()
-    layer_b(1, res, 0, boxes_of((0, 2), NYL))
-    send_out(1, res, 0, 0)
+    for y in (0, 16):
+        for x in (0, 2):
+            layer_b(1, res, 0, boxes_of((x,), y + 16, y))
+            send_out(1, res, 0, x, y)
     drain(0, f1, eb1)
     drain(1, f2, eb2)
 
     for q in range(2):
-        @pl.when(seg == q)
-        def _(q=q):
-            pltpu.make_async_remote_copy(
-                stage.at[q], out.at[1 - seg], sso.at[q], rso.at[q],
-                device_id={"segment": 1 - seg}, device_id_type=MESH).wait_recv()
-        @pl.when(seg != q)
-        def _(q=q):
-            ocopy(q).wait_send()
+        for y in (0, 16):
+            for x in (0, 2):
+                @pl.when(seg == q)
+                def _(q=q, x=x, y=y):
+                    lcopy(q, x, y).wait()
+                    ocopy(q, x, y, 1 - seg).wait_recv()
+                @pl.when(seg != q)
+                def _(q=q, x=x, y=y):
+                    ocopy(q, x, y).wait_send()
 
 
 def shards(sizes, features, weights, biases):
@@ -478,10 +500,10 @@
             pltpu.VMEM((NXL, NYL, C, L), BF),
             pltpu.VMEM((2, C, NXL, NYL, L), BF),
             dma((3,)), dma((2,)), dma((2,)),
-            dma((2, 2, 2, 4)), dma((2, 2, 2, 4)),
+            dma((2, 2, 2, 5)), dma((2, 2, 2, 5)),
             dma((2, 2, NXL)), dma((2, 2, NXL)),
             dma((2, 2, 2, NXL)), dma((2, 2, 2, NXL)),
-            dma((2, NXL)), dma((2, NXL)), dma((2,)), dma((2,)),
+            dma((2, NXL)), dma((2, NXL)), dma((2, 4)), dma((2, 4)), dma((2, 4)),
         ],
         compiler_params=pltpu.CompilerParams(
             collective_id=0, has_side_effects=True, vmem_limit_bytes=32 << 20),

time: 34.6 us -> 35.8 us (1.035)
  Pallas kernels: 33.6 us -> 34.8 us
    pallas_call x1, Pallas kernels: 33.6 us -> 34.8 us  [shards(): pl.pallas_call(functools.partial(kernel, sizes), name='sections', out_sha...]
where the time goes in v5:
time: 35.8 us; the launch traced here: 35.7 us
  Pallas kernels  34.8 us (97%)
  local copies, waits for them, and re-layouts  0.97 us (3%)
    pallas_call x1, Pallas kernels, shards(): pl.pallas_call(functools.partial(kernel, sizes), name='sections', out_sha...  34.8 us
    unnamed x1, local copies, waits for them, and re-layouts  0.97 us

profile of v5, /device:TPU:7, one launch (start us, length us, event | category | flops | bytes accessed | tf_op | source)
XLA Modules:
  0.0 35.7 jit_solution(14748445514960599878)
XLA Ops:
  0.0 34.8 %sections.1 = bf16[2,16,4,32,128]{4,3,2,1,0:T(8,128)(2,1)S(1)} custom-call(bf16[2,16,4,32,128]{4,3,2,1,0:T(8,128)(2,1)} %feat.1, bf16[2,27,16,16]{3,2,1,0:T(8,128)(2,1)} %bitcast.8, bf16[2,16]{1,0:T(2,128)(2,1)} %bitcast.9), custom_call_target="tpu_custom_call" | custom-call | tf_op jit(solution)/shard_map/sections/pallas_call | solution.py:470
  34.8 1.0 %copy.5 = bf16[1,2,16,4,32,128]{5,4,3,2,1,0:T(8,128)(2,1)} copy(bf16[1,2,16,4,32,128]{5,4,3,2,1,0:T(8,128)(2,1)S(1)} %bitcast.7) | data formatting | bytes 2097152
